TPU v7x, 32 devices: a whole 2x2x4 slice. The times are simulated.
32 devices in a mesh: face: 16 (over z, y, core), sub: 2 (over x).
Axes of the slice: x: 2, y: 2, z: 4, core: 2. Of those that a mesh axis runs over, the one named last changes fastest.
Arguments:
- prognostic: bfloat16 [3, 2048, 16, 128], P(None, ('face', 'sub')), may hold values from -4 to 4
- metric: float32 [4, 2048, 16], P(None, ('face', 'sub')), may hold values from -0.35 to 1.6, as said below
- coriolis: float32 [2048, 16], P(('face', 'sub')), may hold values from -1.5 to 1.5
- node_point: int32 [2048, 16], P(('face', 'sub')), may hold values from 0 to 678, as said below
- send_point: int32 [6784], P(('face', 'sub')), may hold values from 0 to 678, as said below
- recv_point: int32 [6784], P(('face', 'sub')), may hold values from 0 to 678, as said below
Outputs:
- advanced: bfloat16 [3, 2048, 16, 128], P(None, ('face', 'sub'))
Inputs may be any that keep to these rules, and one draw needn't show every extreme that they name: `node_point`: each device's numbers are its 679 local points; element nodes that are the same point of the surface on one device carry the same number. `send_point`: on every device the 212 slots form groups in this order: 7 slots of offset +1, 7 of offset -1, 97 of offset +8, 97 of offset -8, then one slot each of offsets 8 + 1, -8 - 1, 7, 1 - 8. A slot names the sender's point that the device at curve index d + o, taken modulo 32, shares. Every slot is used. `recv_point`: slot s of device d names the local point that is the same surface point as the sender's slot s, the sender being the device at d minus the slot's group offset modulo 32. The copies of every shared point are linked between every two devices that hold them. `metric`: entries 0 and 3 lie in [0.6, 1.6], entries 1 and 2 in [-0.35, 0.35].
All inputs are finite; a program needn't handle non-finite values.
Results may differ from a plain program's by a relative error of at most 0.007.
Values sent between devices are 32-bit elements; how exact they have to be, the bound alone decides.
No kernel may reach another device: no remote copies, remote signals or barrier semaphores. Data moves between devices by JAX's collectives and lax.ppermute only.
A program may use at most 64 MiB of HBM per device.

v0:
```python
import math

import jax
import jax.numpy as jnp
import numpy as np
from jax import lax
from jax.experimental import pallas as pl
from jax.experimental.pallas import tpu as pltpu
from jax.sharding import PartitionSpec as P


STEP_SIZE = 0.1
AXES = ("face", "sub")
NODES = 16
SUB = 8
LANES = 128
MASS = 3 * LANES
MIB = 1024 * 1024
CARRIED = {0: (4, 7), 1: (6, 5)}
PASSED = ((4, 6), (7, 5))


def shift(value, steps):
    count = lax.axis_size(AXES)
    return lax.ppermute(value, AXES, [(d, (d + steps) % count) for d in range(count)])


def gll_tables():
    abscissa = np.array([-1.0, -math.sqrt(0.2), math.sqrt(0.2), 1.0])
    legendre = 0.5 * (5.0 * abscissa * abscissa * abscissa - 3.0 * abscissa)
    derivative = np.zeros((4, 4))
    for target in range(4):
        for source in range(4):
            if target != source:
                derivative[target, source] = legendre[target] / (
                    legendre[source] * (abscissa[target] - abscissa[source])
                )
    derivative[0, 0] = -3.0
    derivative[3, 3] = 3.0
    weights = np.array([1.0, 5.0, 5.0, 1.0]) / 6.0
    return (derivative, weights)


class Plan:
    def __init__(self, elements, links, lap):
        around = (links - 8) // 6
        short = 1
        while short * (around - short) < elements:
            short += 1
        side = 3 * short + 1
        top = 3 * (around - short) + 1
        first = [0]
        for count in (side, side, top, top, 1, 1, 1):
            first.append(first[-1] + count)
        self.offsets = (1, -1, lap, -lap, lap + 1, -lap - 1, lap - 1, 1 - lap)
        self.lap = lap
        self.tiles = top // SUB * SUB
        self.rest = top - self.tiles
        self.side_rows = -(-side // SUB) * SUB
        self.sides = 2 * self.tiles
        self.tail = self.sides + 2 * self.side_rows
        self.corner = self.tail + 2 * self.rest
        self.rows = -(-(self.corner + 4) // SUB) * SUB
        self.width = -(-self.rows // 256) * 256
        self.weight_rows = self.width // LANES
        self.spans = []
        for group in range(8):
            start = first[group]
            if group < 2:
                spans = ((start, self.sides + group * self.side_rows, side),)
            elif group < 4:
                spans = (
                    (start, (group - 2) * self.tiles, self.tiles),
                    (start + self.tiles, self.tail + (group - 2) * self.rest, self.rest),
                )
            else:
                spans = ((start, self.corner + group - 4, 1),)
            self.spans.append([span for span in spans if span[2]])

    def blocks(self, group):
        out = []
        place = 0
        for _, row, count in self.spans[group]:
            pitch = self.side_rows if group < 2 else count
            out.append((row, place, count, pitch))
            place += 3 * pitch
        for passed in CARRIED.get(group, ()):
            out.append((self.corner + passed - 4, place, 1, 1))
            place += 3
        return out

    def weight_row(self, group):
        _, place, _, pitch = self.blocks(group)[-1]
        return place + 3 * pitch

    def message_rows(self, group):
        return -(-(self.weight_row(group) + self.weight_rows) // SUB) * SUB

    def lanes(self, groups, index):
        at = iota((1, LANES), 1) + index * LANES
        mine = at < 0
        for group in groups:
            for _, row, count in self.spans[group]:
                mine = mine | ((at >= row) & (at < row + count))
        return mine


def iota(shape, axis):
    return lax.broadcasted_iota(jnp.int32, shape, axis)


def arranged(points_ref, plan):
    links = points_ref.shape[1]
    width = plan.width
    raw = points_ref[...].astype(jnp.float32)
    raw = jnp.concatenate([raw, jnp.full((1, width - links), -1.0, jnp.float32)], axis=1)
    raw = jnp.broadcast_to(raw, (SUB, width))
    lane = iota((SUB, width), 1)
    row = jnp.full((SUB, width), -1.0, jnp.float32)
    for spans in plan.spans:
        for source, target, count in spans:
            turned = pltpu.roll(raw, (target - source) % width, 1)
            row = jnp.where((lane >= target) & (lane < target + count), turned, row)
    return row[0:1]


def as_column(row, rows):
    width = row.shape[1]
    shape = (rows, width)
    return jnp.sum(jnp.where(iota(shape, 0) == iota(shape, 1), row, 0.0), axis=1, keepdims=True)


def as_row(column, width):
    shape = (column.shape[0], width)
    return jnp.sum(jnp.where(iota(shape, 0) == iota(shape, 1), column[:, :1], 0.0), axis=0, keepdims=True)


def point_rows(stack, first):
    elements = stack.shape[0]
    square = (LANES, LANES)
    spread = (iota(square, 1) // SUB + first == iota(square, 0)).astype(jnp.float32)
    wide = jnp.dot(stack, spread, precision=lax.Precision.HIGHEST, preferred_element_type=jnp.float32)
    mine = iota(wide.shape, 1) % SUB == iota(wide.shape, 0) % SUB
    return jnp.sum(jnp.where(mine, wide, 0.0).reshape(elements // SUB, SUB, LANES), axis=1)


def both_halves(mass):
    return mass + pltpu.roll(mass, LANES // 2, 1)


def split_lanes(mass):
    upper = mass.astype(jnp.bfloat16).astype(jnp.float32)
    return jnp.where(iota(mass.shape, 1) < LANES // 2, mass, mass - upper)


def derive(values, axis, scale):
    table, _ = gll_tables()
    out = [None] * NODES
    for other in range(4):
        spot = (lambda i: 4 * other + i) if axis == 1 else (lambda i: 4 * i + other)
        x0, x1, x2, x3 = (values[spot(i)] for i in range(4))
        diff_a = x0 - x3
        diff_b = x1 - x2
        even = (x0 + x3) - (x1 + x2)
        for i in (0, 1):
            factor = scale[other] * scale[i]
            p = even * np.float32(factor * 0.5 * (table[i, 0] + table[i, 3]))
            q = diff_a * np.float32(factor * 0.5 * (table[i, 0] - table[i, 3])) + diff_b * np.float32(
                factor * 0.5 * (table[i, 1] - table[i, 2])
            )
            out[spot(i)] = q + p
            out[spot(3 - i)] = q - p
    return out


def tendency_kernel(plan, *refs):
    prog, metric, cor, points, send, recv = refs[:6]
    fields, weighted, numbers, pts_v, recv_v = refs[6:11]
    messages = refs[11:15]
    met_v, cor_v, send_v, tile, mask, coefs, sems, chunk_sems = refs[15:]
    elements = fields.shape[1]
    groups = elements // SUB
    chunks = chunk_sems.shape[0]
    per = elements // chunks
    smalls = [
        pltpu.make_async_copy(source, target, sems.at[i])
        for i, (source, target) in enumerate(((points, pts_v), (send, send_v), (metric, met_v), (cor, cor_v)))
    ]
    for copy in smalls:
        copy.start()
    larges = [
        pltpu.make_async_copy(
            prog.at[:, pl.ds(i * per, per)], fields.at[:, pl.ds(i * per, per)], chunk_sems.at[i]
        )
        for i in range(chunks)
    ]
    for copy in larges:
        copy.start()
    later = pltpu.make_async_copy(recv, recv_v, sems.at[4])
    later.start()
    for copy in smalls:
        copy.wait()
    rows = plan.rows
    wanted = as_column(arranged(send_v, plan), rows)
    _, scale = gll_tables()
    a, b, e, g = (met_v[i] for i in range(4))
    node = iota(a.shape, 0)
    row_edge = (node // 4 == 0) | (node // 4 == 3)
    col_edge = (node % 4 == 0) | (node % 4 == 3)
    quad = jnp.where(row_edge, np.float32(scale[0]), np.float32(scale[1])) * jnp.where(
        col_edge, np.float32(scale[0]), np.float32(scale[1])
    )
    inv = 1.0 / (a * g - b * e)
    mass = quad * inv
    stack = (a * inv, b * inv, e * inv, g * inv, mass * cor_v[...], mass, pts_v[...].astype(jnp.float32))
    spare = LANES - len(stack) * NODES
    stack = jnp.concatenate(stack + (jnp.zeros((spare, elements), jnp.float32),), axis=0)
    coefs[...] = jnp.transpose(stack)
    numbers[...] = point_rows(coefs[...], 6 * NODES)
    for group in range(groups):
        mask[:, group * LANES : (group + 1) * LANES] = (
            jnp.broadcast_to(wanted, (rows, LANES)) == numbers[group : group + 1, :]
        ).astype(jnp.bfloat16)

    def body(group, carry):
        here = pl.ds(group * SUB, SUB)
        compact = coefs[here, :]

        def spread(which):
            lanes = range(which * NODES, (which + 1) * NODES)
            return [jnp.broadcast_to(compact[:, k : k + 1], (SUB, LANES)) for k in lanes]

        ca, cb, ce, cg, cf, cm = (spread(i) for i in range(6))
        for f in range(3):
            tile[f] = fields[f, here].astype(jnp.float32).reshape(SUB * NODES, LANES)
        u, v, h = ([tile[f, pl.ds(k, SUB, stride=NODES), :] for k in range(NODES)] for f in range(3))
        span = range(NODES)
        energy = [0.5 * (u[k] * u[k] + v[k] * v[k]) + h[k] for k in span]
        along = derive(energy, 1, scale)
        across = derive(energy, 0, scale)
        grad_one = [ca[k] * along[k] + ce[k] * across[k] for k in span]
        grad_two = [cb[k] * along[k] + cg[k] * across[k] for k in span]
        turn_two = derive([ca[k] * v[k] - cb[k] * u[k] for k in span], 1, scale)
        turn_one = derive([cg[k] * u[k] - ce[k] * v[k] for k in span], 0, scale)
        eta = [turn_two[k] - turn_one[k] + cf[k] for k in span]
        flow_one = derive([h[k] * (ca[k] * u[k] + cb[k] * v[k]) for k in span], 1, scale)
        flow_two = derive([h[k] * (ce[k] * u[k] + cg[k] * v[k]) for k in span], 0, scale)
        parts = (
            [eta[k] * v[k] - grad_one[k] for k in span],
            [-(eta[k] * u[k]) - grad_two[k] for k in span],
            [-(flow_one[k] + flow_two[k]) for k in span],
            [split_lanes(cm[k]) for k in span],
        )
        there = pl.ds(group * LANES, LANES)
        for f, part in enumerate(parts):
            weighted[there, f * LANES : (f + 1) * LANES] = jnp.concatenate(part, axis=0).astype(jnp.bfloat16)
        return carry

    step = groups // chunks
    for i in range(chunks):
        larges[i].wait()
        lax.fori_loop(i * step, (i + 1) * step, body, 0)
    later.wait()
    sums = jnp.dot(mask[...], weighted[...], preferred_element_type=jnp.float32)
    masses = as_row(both_halves(sums[:, MASS:]), plan.width)
    for group, ref in enumerate(messages):
        ref[ref.shape[0] - SUB :, :] = jnp.zeros((SUB, LANES), jnp.float32)
        for row, place, count, pitch in plan.blocks(group):
            span = pitch if pitch > count else count
            for f in range(3):
                ref[place + f * pitch : place + f * pitch + span, :] = sums[
                    row : row + span, f * LANES : (f + 1) * LANES
                ]
        for index in range(plan.weight_rows):
            mine = plan.lanes((group, *CARRIED.get(group, ())), index)
            at = plan.weight_row(group) + index
            ref[at : at + 1, :] = jnp.where(mine, masses[:, index * LANES : (index + 1) * LANES], 0.0)


def point_columns(points, group):
    return jnp.concatenate(
        [
            jnp.broadcast_to(points[:, e : e + 1], (NODES, LANES))
            for e in range(group * SUB, (group + 1) * SUB)
        ],
        axis=0,
    )


def local_sums(points, numbers, weighted, own):
    groups = weighted.shape[0] // LANES
    tall = SUB * NODES
    for i in range(own.shape[0] // tall):
        column = point_columns(points, i)
        same = jnp.concatenate(
            [(column == numbers[j : j + 1, :]).astype(jnp.bfloat16) for j in range(groups)], axis=1
        )
        own[i * tall : (i + 1) * tall, :] = jnp.dot(same, weighted[...], preferred_element_type=jnp.float32)


def local_kernel(plan, weighted, numbers, points, recv, own, table):
    landing = arranged(recv, plan)
    values = points[...].astype(jnp.float32)
    tall = SUB * NODES
    for group in range(numbers.shape[0]):
        column = point_columns(values, group)
        for i in range(0, plan.width, LANES):
            table[group * tall : (group + 1) * tall, i : i + LANES] = (
                column == landing[:, i : i + LANES]
            ).astype(jnp.bfloat16)
    local_sums(values, numbers, weighted, own)


def relay_kernel(plan, left, right, own, up, down):
    start = plan.weight_row(0)
    for i, ref in enumerate((up, down)):
        place = plan.blocks(0)[-2 + i][1]
        ref[0:3, :] = left[place : place + 3, :]
        ref[3:6, :] = right[place : place + 3, :]
        for index in range(plan.weight_rows):
            at = slice(start + index, start + index + 1)
            ref[6 + index : 7 + index, :] = jnp.where(
                plan.lanes(PASSED[i][:1], index), left[at, :], 0.0
            ) + jnp.where(plan.lanes(PASSED[i][1:], index), right[at, :], 0.0)


def finish_kernel(plan, fields, own, table, *refs):
    messages = refs[:4]
    relays = refs[4:6]
    out, held, landed, sems = refs[6:]
    width = plan.width
    landed[plan.tail :, :] = jnp.zeros((width - plan.tail, landed.shape[1]), jnp.float32)
    weights = []
    for index in range(plan.weight_rows):
        parts = [ref[6 + index : 7 + index, :] for ref in relays]
        for group, ref in enumerate(messages):
            at = plan.weight_row(group) + index
            row = ref[at : at + 1, :]
            parts.append(jnp.where(plan.lanes((group,), index), row, 0.0) if group < 2 else row)
        weights.append(sum(parts[1:], parts[0]))
    masses = as_column(jnp.concatenate(weights, axis=1), width)
    for group, ref in enumerate(messages):
        for row, place, count, pitch in plan.blocks(group)[: len(plan.spans[group])]:
            span = pitch if pitch > count else count
            for f in range(3):
                landed[row : row + span, f * LANES : (f + 1) * LANES] = ref[
                    place + f * pitch : place + f * pitch + span, :
                ]
    for passed, ref in zip(PASSED, relays):
        for i, group in enumerate(passed):
            row = plan.corner + group - 4
            for f in range(3):
                landed[row : row + 1, f * LANES : (f + 1) * LANES] = ref[3 * i + f : 3 * i + f + 1, :]
    landed[:, MASS:] = split_lanes(jnp.broadcast_to(masses, (width, LANES)))
    arrived = landed[...].astype(jnp.bfloat16)
    chunks = sems.shape[0]
    elements = fields.shape[1]
    per = elements // chunks
    copies = []
    for i in range(chunks):
        rows = slice(i * per * NODES, (i + 1) * per * NODES)
        here = slice(i * per, (i + 1) * per)
        total = own[rows, :] + jnp.dot(table[rows, :], arrived, preferred_element_type=jnp.float32)
        factor = np.float32(STEP_SIZE) / both_halves(total[:, MASS:])
        for f in range(3):
            moved = (total[:, f * LANES : (f + 1) * LANES] * factor).reshape(per, NODES, LANES)
            held[f, here] = (fields[f, here].astype(jnp.float32) + moved).astype(jnp.bfloat16)
        copy = pltpu.make_async_copy(
            held.at[:, pl.ds(i * per, per)], out.at[:, pl.ds(i * per, per)], sems.at[i]
        )
        copy.start()
        copies.append(copy)
    for copy in copies:
        copy.wait()


def in_hbm(value):
    return pltpu.with_memory_space_constraint(value, pltpu.HBM)


def call(kernel, outs, ins, args, scratch=(), limit=8 * MIB, flops=0):
    return pl.pallas_call(
        kernel,
        out_shape=[jax.ShapeDtypeStruct(shape, dtype) for shape, dtype, _ in outs],
        out_specs=[pl.BlockSpec(memory_space=space) for _, _, space in outs],
        in_specs=[pl.BlockSpec(memory_space=space) for space in ins],
        scratch_shapes=list(scratch),
        compiler_params=pltpu.CompilerParams(vmem_limit_bytes=limit),
        cost_estimate=pl.CostEstimate(flops=flops, bytes_accessed=0, transcendentals=0) if flops else None,
    )(*args)


def local(prognostic, metric, coriolis, node_point, send_point, recv_point):
    elements = prognostic.shape[1]
    levels = prognostic.shape[3]
    links = send_point.shape[0]
    plan = Plan(elements, links, 4 * lax.axis_size("sub"))
    rows = elements * NODES
    vm, hbm = pltpu.VMEM, pltpu.HBM
    f32, bf16 = jnp.float32, jnp.bfloat16
    send = send_point.reshape(1, links)
    recv = recv_point.reshape(1, links)
    metric = jnp.transpose(metric, (0, 2, 1))
    coriolis = jnp.transpose(coriolis)
    points = jnp.transpose(node_point)
    wide = 4 * levels
    sent = call(
        lambda *refs: tendency_kernel(plan, *refs),
        (
            (prognostic.shape, bf16, vm),
            ((rows, wide), bf16, vm),
            ((elements // SUB, LANES), f32, vm),
            (points.shape, jnp.int32, vm),
            (recv.shape, jnp.int32, vm),
        )
        + tuple(((plan.message_rows(group), LANES), f32, vm) for group in range(4)),
        (hbm,) * 6,
        tuple(in_hbm(x) for x in (prognostic, metric, coriolis, points, send, recv)),
        (
            vm(metric.shape, f32),
            vm(coriolis.shape, f32),
            vm(send.shape, jnp.int32),
            vm((3, SUB * NODES, levels), f32),
            vm((plan.rows, rows), bf16),
            vm((elements, LANES), f32),
            pltpu.SemaphoreType.DMA((5,)),
            pltpu.SemaphoreType.DMA((4,)),
        ),
    )
    fields, weighted, numbers, points, recv = sent[:5]
    landed = []
    for group in range(4):
        landed.append(shift(sent[5 + group], plan.offsets[group]))
    own, table = call(
        lambda *refs: local_kernel(plan, *refs),
        (((rows, wide), f32, vm), ((rows, plan.width), bf16, vm)),
        (vm,) * 4,
        (weighted, numbers, points, recv),
    )
    relays = call(
        lambda *refs: relay_kernel(plan, *refs),
        (((SUB, LANES), f32, vm),) * 2,
        (vm, vm, pl.ANY),
        (landed[0], landed[1], own),
    )
    passed = []
    for i, offset in enumerate((plan.lap, -plan.lap)):
        passed.append(shift(relays[i], offset))
    (advanced,) = call(
        lambda *refs: finish_kernel(plan, *refs),
        ((prognostic.shape, bf16, hbm),),
        (vm,) * 9,
        (fields, own, table, *landed, *passed),
        (
            vm(prognostic.shape, bf16),
            vm((plan.width, wide), f32),
            pltpu.SemaphoreType.DMA((4,)),
        ),
    )
    return advanced


def solution(mesh):
    placed = (
        P(None, AXES, None, None),
        P(None, AXES, None),
        P(AXES, None),
        P(AXES, None),
        P(AXES),
        P(AXES),
    )
    return jax.shard_map(
        local,
        mesh=mesh,
        in_specs=placed,
        out_specs=P(None, AXES, None, None),
        check_vma=False,
    )
```

profile of v0, /device:TPU:0, one launch (start us, length us, event | category | flops | bytes accessed | tf_op | source)
XLA Modules:
  0.0 24.4 jit_solution(13083702481471058266)
XLA Ops:
  0.0 4.0 %shard_map.64 = (bf16[3,64,16,128]{3,2,1,0:T(8,128)(2,1)S(1)}, bf16[1024,512]{1,0:T(8,128)(2,1)S(1)}, f32[8,128]{1,0:T(8,128)S(1)}, s32[16,64]{1,0:T(8,128)S(1)}...) custom-call(bf16[3,64,16,128]{3,2,1,0:T(8,128)(2,1)} %refs_0_.1, ...), custom_call_target="tpu_custom_call" | custom-call | tf_op jit(solution)/shard_map/pallas_call | solution.py:382
  4.0 3.1 %collective-permute-start.2 = (f32[296,128]{1,0:T(8,128)S(1)}, f32[296,128]{1,0:T(8,128)S(1)}, u32[]{:S(2)}, u32[]{:S(2)}) collective-permute-start(f32[296,128]{1,0:T(8,128)S(1)} %get-tuple-element.27), channel_id=1, source_target_pairs={{0,8},{1,9},{2,10},{3,11},{4,12},{5,13},{6,14},{7,15},{8,16},{9,17... | collective-permute-start | bytes 454664 | tf_op jit(solution)/shard_map/ppermute | solution.py:25
  7.1 2.1 %collective-permute-start.3 = (f32[296,128]{1,0:T(8,128)S(1)}, f32[296,128]{1,0:T(8,128)S(1)}, u32[]{:S(2)}, u32[]{:S(2)}) collective-permute-start(f32[296,128]{1,0:T(8,128)S(1)} %get-tuple-element.28), channel_id=1, source_target_pairs={{0,24},{1,25},{2,26},{3,27},{4,28},{5,29},{6,30},{7,31},{8,0},{9,1... | collective-permute-start | bytes 454664 | tf_op jit(solution)/shard_map/ppermute | solution.py:25
  9.2 1.6 %collective-permute-start = (f32[32,128]{1,0:T(8,128)S(1)}, f32[32,128]{1,0:T(8,128)S(1)}, u32[]{:S(2)}, u32[]{:S(2)}) collective-permute-start(f32[32,128]{1,0:T(8,128)S(1)} %get-tuple-element.25), channel_id=1, source_target_pairs={{0,1},{1,2},{2,3},{3,4},{4,5},{5,6},{6,7},{7,8},{8,9},{9,10},{10,1... | collective-permute-start | bytes 49160 | tf_op jit(solution)/shard_map/ppermute | solution.py:25
  10.9 3.7 %collective-permute-start.1 = (f32[32,128]{1,0:T(8,128)S(1)}, f32[32,128]{1,0:T(8,128)S(1)}, u32[]{:S(2)}, u32[]{:S(2)}) collective-permute-start(f32[32,128]{1,0:T(8,128)S(1)} %get-tuple-element.26), channel_id=1, source_target_pairs={{0,31},{1,0},{2,1},{3,2},{4,3},{5,4},{6,5},{7,6},{8,7},{9,8},{10,9... | collective-permute-start | bytes 49160 | tf_op jit(solution)/shard_map/ppermute | solution.py:25
  14.6 1.4 %shard_map.65 = (f32[1024,512]{1,0:T(8,128)S(1)}, bf16[1024,256]{1,0:T(8,128)(2,1)S(1)}) custom-call(bf16[1024,512]{1,0:T(8,128)(2,1)S(1)} %get-tuple-element.19.refs_0_, f32[8,128]{1,0:T(8,128)S(1)} %get-tuple-element.20.refs_1_, s32[16,64]{1,0:T(8,128)S(1)} %get-tuple-element.21.refs_2_, s32[1,212]{1,0:T(1,128)S(1)} %get-tuple-element.22.refs_3_), custom_call_target="tpu_custom_call" | custom-call | tf_op jit(solution)/shard_map/pallas_call | solution.py:382
  16.0 1.6 %collective-permute-done.refs_0_.refs_3_ = f32[32,128]{1,0:T(8,128)S(1)} collective-permute-done((f32[32,128]{1,0:T(8,128)S(1)}, f32[32,128]{1,0:T(8,128)S(1)}, u32[]{:S(2)}, u32[]{:S(2)}) %collective-permute-start) | collective-permute-done | bytes 16416 | tf_op jit(solution)/shard_map/ppermute | solution.py:25
  17.5 0.0 collective-permute-done.1.refs_1_.refs_4_
  17.5 0.1 collective-permute-start.4
  17.6 3.8 %collective-permute-start.5 = (f32[8,128]{1,0:T(8,128)S(1)}, f32[8,128]{1,0:T(8,128)S(1)}, u32[]{:S(2)}, u32[]{:S(2)}) collective-permute-start(f32[8,128]{1,0:T(8,128)S(1)} %get-tuple-element.30), channel_id=1, source_target_pairs={{0,24},{1,25},{2,26},{3,27},{4,28},{5,29},{6,30},{7,31},{8,0},{9,1... | collective-permute-start | bytes 12296 | tf_op jit(solution)/shard_map/ppermute | solution.py:25
  21.4 1.6 %collective-permute-done.4.refs_7_ = f32[8,128]{1,0:T(8,128)S(1)} collective-permute-done((f32[8,128]{1,0:T(8,128)S(1)}, f32[8,128]{1,0:T(8,128)S(1)}, u32[]{:S(2)}, u32[]{:S(2)}) %collective-permute-start.4) | collective-permute-done | bytes 4128 | tf_op jit(solution)/shard_map/ppermute | solution.py:25
  23.0 0.0 collective-permute-done.5.refs_8_
  23.0 0.0 collective-permute-done.2.refs_5_
  23.0 0.0 collective-permute-done.3.refs_6_
  23.0 1.4 %shard_map.67 = bf16[3,64,16,128]{3,2,1,0:T(8,128)(2,1)} custom-call(bf16[3,64,16,128]{3,2,1,0:T(8,128)(2,1)S(1)} %get-tuple-element.18.refs_0_, f32[1024,512]{1,0:T(8,128)S(1)} %get-tuple-element.23.refs_2_.refs_1_, bf16[1024,256]{1,0:T(8,128)(2,1)S(1)} %get-tuple-element.24.refs_2_, f32[32,128]{1,0:T(8,128)S(1)} %collective-permute-done.refs_0_.refs_3_, ...), custom_call_target="tpu_custom_call" | custom-call | tf_op jit(solution)/shard_map/pallas_call | solution.py:382
  (1 shorter events, 0.0 us)
Async XLA Ops:
  4.0 19.0 %collective-permute-start.2 = (f32[296,128]{1,0:T(8,128)S(1)}, f32[296,128]{1,0:T(8,128)S(1)}, u32[]{:S(2)}, u32[]{:S(2)}) collective-permute-start(f32[296,128]{1,0:T(8,128)S(1)} %get-tuple-element.27), channel_id=1, source_target_pairs={{0,8},{1,9},{2,10},{3,11},{4,12},{5,13},{6,14},{7,15},{8,16},{9,17... | collective-permute-start | bytes 454664 | tf_op jit(solution)/shard_map/ppermute | solution.py:25
  7.1 15.9 %collective-permute-start.3 = (f32[296,128]{1,0:T(8,128)S(1)}, f32[296,128]{1,0:T(8,128)S(1)}, u32[]{:S(2)}, u32[]{:S(2)}) collective-permute-start(f32[296,128]{1,0:T(8,128)S(1)} %get-tuple-element.28), channel_id=1, source_target_pairs={{0,24},{1,25},{2,26},{3,27},{4,28},{5,29},{6,30},{7,31},{8,0},{9,1... | collective-permute-start | bytes 454664 | tf_op jit(solution)/shard_map/ppermute | solution.py:25
  9.2 8.3 %collective-permute-start = (f32[32,128]{1,0:T(8,128)S(1)}, f32[32,128]{1,0:T(8,128)S(1)}, u32[]{:S(2)}, u32[]{:S(2)}) collective-permute-start(f32[32,128]{1,0:T(8,128)S(1)} %get-tuple-element.25), channel_id=1, source_target_pairs={{0,1},{1,2},{2,3},{3,4},{4,5},{5,6},{6,7},{7,8},{8,9},{9,10},{10,1... | collective-permute-start | bytes 49160 | tf_op jit(solution)/shard_map/ppermute | solution.py:25
  10.9 6.7 %collective-permute-start.1 = (f32[32,128]{1,0:T(8,128)S(1)}, f32[32,128]{1,0:T(8,128)S(1)}, u32[]{:S(2)}, u32[]{:S(2)}) collective-permute-start(f32[32,128]{1,0:T(8,128)S(1)} %get-tuple-element.26), channel_id=1, source_target_pairs={{0,31},{1,0},{2,1},{3,2},{4,3},{5,4},{6,5},{7,6},{8,7},{9,8},{10,9... | collective-permute-start | bytes 49160 | tf_op jit(solution)/shard_map/ppermute | solution.py:25
  17.5 5.5 %collective-permute-start.4 = (f32[8,128]{1,0:T(8,128)S(1)}, f32[8,128]{1,0:T(8,128)S(1)}, u32[]{:S(2)}, u32[]{:S(2)}) collective-permute-start(f32[8,128]{1,0:T(8,128)S(1)} %get-tuple-element.29), channel_id=1, source_target_pairs={{0,8},{1,9},{2,10},{3,11},{4,12},{5,13},{6,14},{7,15},{8,16},{9,17... | collective-permute-start | bytes 12296 | tf_op jit(solution)/shard_map/ppermute | solution.py:25
  17.6 5.4 %collective-permute-start.5 = (f32[8,128]{1,0:T(8,128)S(1)}, f32[8,128]{1,0:T(8,128)S(1)}, u32[]{:S(2)}, u32[]{:S(2)}) collective-permute-start(f32[8,128]{1,0:T(8,128)S(1)} %get-tuple-element.30), channel_id=1, source_target_pairs={{0,24},{1,25},{2,26},{3,27},{4,28},{5,29},{6,30},{7,31},{8,0},{9,1... | collective-permute-start | bytes 12296 | tf_op jit(solution)/shard_map/ppermute | solution.py:25
where the time goes:
time: 24.6 us; the launch traced here: 24.4 us
  starting transfers between devices  14.4 us (59%)
  Pallas kernels  6.81 us (28%)
  waiting for transfers between devices  3.15 us (13%)
    ppermute x6, starting transfers between devices, shift(): lax.ppermute(value, AXES, [(d, (d + steps) % count) for d in range(count)])  14.4 us
    pallas_call x4, Pallas kernels, call(): pl.pallas_call(kernel, out_shape=[jax.ShapeDtypeStruct(shape, dtype) for...  6.81 us
    ppermute x6, waiting for transfers between devices, shift(): lax.ppermute(value, AXES, [(d, (d + steps) % count) for d in range(count)])  3.15 us
  transfers between devices with their start and end apart: 6, of which 2 were waited for; matrix products, arithmetic and copies ran while one was open for 0% of the time, Pallas kernels for 6%

commit v1 on v0

--- a/solution.py
+++ b/solution.py
@@ -153,7 +153,7 @@
     return jnp.where(iota(mass.shape, 1) < LANES // 2, mass, mass - upper)
 
 
-def derive(values, axis, scale):
+def derive(values, axis, scale, sign=1.0):
     table, _ = gll_tables()
     out = [None] * NODES
     for other in range(4):
@@ -163,7 +163,7 @@
         diff_b = x1 - x2
         even = (x0 + x3) - (x1 + x2)
         for i in (0, 1):
-            factor = scale[other] * scale[i]
+            factor = sign * scale[other] * scale[i]
             p = even * np.float32(factor * 0.5 * (table[i, 0] + table[i, 3]))
             q = diff_a * np.float32(factor * 0.5 * (table[i, 0] - table[i, 3])) + diff_b * np.float32(
                 factor * 0.5 * (table[i, 1] - table[i, 2])
@@ -177,7 +177,7 @@
     prog, metric, cor, points, send, recv = refs[:6]
     fields, weighted, numbers, pts_v, recv_v = refs[6:11]
     messages = refs[11:15]
-    met_v, cor_v, send_v, tile, mask, coefs, sems, chunk_sems = refs[15:]
+    met_v, cor_v, send_v, tile, mask, total, coefs, sems, chunk_sems = refs[15:]
     elements = fields.shape[1]
     groups = elements // SUB
     chunks = chunk_sems.shape[0]
@@ -194,12 +194,13 @@
         )
         for i in range(chunks)
     ]
-    for copy in larges:
-        copy.start()
+    larges[0].start()
     later = pltpu.make_async_copy(recv, recv_v, sems.at[4])
     later.start()
     for copy in smalls:
         copy.wait()
+    for copy in larges[1:]:
+        copy.start()
     rows = plan.rows
     wanted = as_column(arranged(send_v, plan), rows)
     _, scale = gll_tables()
@@ -212,56 +213,93 @@
     )
     inv = 1.0 / (a * g - b * e)
     mass = quad * inv
-    stack = (a * inv, b * inv, e * inv, g * inv, mass * cor_v[...], mass, pts_v[...].astype(jnp.float32))
-    spare = LANES - len(stack) * NODES
-    stack = jnp.concatenate(stack + (jnp.zeros((spare, elements), jnp.float32),), axis=0)
-    coefs[...] = jnp.transpose(stack)
-    numbers[...] = point_rows(coefs[...], 6 * NODES)
+    upper = mass.astype(jnp.bfloat16).astype(jnp.float32)
+    stack = (a * inv, b * inv, e * inv, g * inv, mass * cor_v[...], upper, mass - upper, pts_v[...].astype(jnp.float32))
+    stack = jnp.transpose(jnp.concatenate(stack, axis=0))
+    numbers[...] = point_rows(stack, 7 * NODES)
+    square = (LANES, LANES)
+    kind = iota(square, 0) // NODES
+    half = (iota(square, 1) >= LANES // 2).astype(jnp.int32)
+    lift = [(kind == i).astype(jnp.bfloat16) for i in range(5)]
+    fine = jnp.concatenate(lift + [jnp.zeros(square, jnp.bfloat16)], axis=1)
+    lift = jnp.concatenate([jnp.concatenate(lift + [(kind == 5 + half).astype(jnp.bfloat16)], axis=1), fine], axis=0)
+    coarse = stack.astype(jnp.bfloat16).astype(jnp.float32)
+    slot = iota((SUB, LANES), 1) % NODES
+    for group in range(groups):
+        here = slice(group * SUB, (group + 1) * SUB)
+        picked = jnp.concatenate(
+            [
+                jnp.concatenate([jnp.where(slot == k, part[here], 0.0) for k in range(NODES)], axis=0)
+                for part in (coarse, stack - coarse)
+            ],
+            axis=1,
+        ).astype(jnp.bfloat16)
+        there = slice(group * LANES, (group + 1) * LANES)
+        wide = jnp.dot(picked, lift, preferred_element_type=jnp.float32)
+        for i in range(5):
+            coefs[i, there, :] = wide[:, i * LANES : (i + 1) * LANES]
+        weighted[there, MASS:] = wide[:, 5 * LANES :].astype(jnp.bfloat16)
     for group in range(groups):
         mask[:, group * LANES : (group + 1) * LANES] = (
             jnp.broadcast_to(wanted, (rows, LANES)) == numbers[group : group + 1, :]
         ).astype(jnp.bfloat16)
 
-    def body(group, carry):
-        here = pl.ds(group * SUB, SUB)
-        compact = coefs[here, :]
-
-        def spread(which):
-            lanes = range(which * NODES, (which + 1) * NODES)
-            return [jnp.broadcast_to(compact[:, k : k + 1], (SUB, LANES)) for k in lanes]
-
-        ca, cb, ce, cg, cf, cm = (spread(i) for i in range(6))
-        for f in range(3):
-            tile[f] = fields[f, here].astype(jnp.float32).reshape(SUB * NODES, LANES)
-        u, v, h = ([tile[f, pl.ds(k, SUB, stride=NODES), :] for k in range(NODES)] for f in range(3))
+    def body(group):
+        ca, cb, ce, cg, cf = (
+            [coefs[i, (group * NODES + k) * SUB : (group * NODES + k + 1) * SUB, :] for k in range(NODES)]
+            for i in range(5)
+        )
+        u, v, h = ([tile[group, f, k * SUB : (k + 1) * SUB, :] for k in range(NODES)] for f in range(3))
         span = range(NODES)
         energy = [0.5 * (u[k] * u[k] + v[k] * v[k]) + h[k] for k in span]
-        along = derive(energy, 1, scale)
-        across = derive(energy, 0, scale)
+        along = derive(energy, 1, scale, -1.0)
+        across = derive(energy, 0, scale, -1.0)
         grad_one = [ca[k] * along[k] + ce[k] * across[k] for k in span]
         grad_two = [cb[k] * along[k] + cg[k] * across[k] for k in span]
         turn_two = derive([ca[k] * v[k] - cb[k] * u[k] for k in span], 1, scale)
         turn_one = derive([cg[k] * u[k] - ce[k] * v[k] for k in span], 0, scale)
         eta = [turn_two[k] - turn_one[k] + cf[k] for k in span]
-        flow_one = derive([h[k] * (ca[k] * u[k] + cb[k] * v[k]) for k in span], 1, scale)
-        flow_two = derive([h[k] * (ce[k] * u[k] + cg[k] * v[k]) for k in span], 0, scale)
+        flow_one = derive([h[k] * (ca[k] * u[k] + cb[k] * v[k]) for k in span], 1, scale, -1.0)
+        flow_two = derive([h[k] * (ce[k] * u[k] + cg[k] * v[k]) for k in span], 0, scale, -1.0)
         parts = (
-            [eta[k] * v[k] - grad_one[k] for k in span],
-            [-(eta[k] * u[k]) - grad_two[k] for k in span],
-            [-(flow_one[k] + flow_two[k]) for k in span],
-            [split_lanes(cm[k]) for k in span],
+            [eta[k] * v[k] + grad_one[k] for k in span],
+            [grad_two[k] - eta[k] * u[k] for k in span],
+            [flow_one[k] + flow_two[k] for k in span],
         )
-        there = pl.ds(group * LANES, LANES)
+        there = slice(group * LANES, (group + 1) * LANES)
         for f, part in enumerate(parts):
             weighted[there, f * LANES : (f + 1) * LANES] = jnp.concatenate(part, axis=0).astype(jnp.bfloat16)
-        return carry
 
     step = groups // chunks
+    turn = (
+        iota(square, 1) == iota(square, 0) % SUB * NODES + iota(square, 0) // SUB
+    ).astype(jnp.bfloat16)
+
+    def reorder(i):
+        larges[i].wait()
+        for group in range(i * step, (i + 1) * step):
+            here = slice(group * SUB, (group + 1) * SUB)
+            for f in range(3):
+                tile[group, f] = jnp.dot(
+                    turn, fields[f, here].reshape(SUB * NODES, LANES), preferred_element_type=jnp.float32
+                )
+
+    def gather(i):
+        span = slice(i * step * LANES, (i + 1) * step * LANES)
+        part = jnp.dot(mask[:, span], weighted[span, :], preferred_element_type=jnp.float32)
+        total[...] = part if i == 0 else total[...] + part
+
+    reorder(0)
     for i in range(chunks):
-        larges[i].wait()
-        lax.fori_loop(i * step, (i + 1) * step, body, 0)
+        if i + 1 < chunks:
+            reorder(i + 1)
+        for group in range(i * step, (i + 1) * step):
+            body(group)
+        if i:
+            gather(i - 1)
+    gather(chunks - 1)
     later.wait()
-    sums = jnp.dot(mask[...], weighted[...], preferred_element_type=jnp.float32)
+    sums = total[...]
     masses = as_row(both_halves(sums[:, MASS:]), plan.width)
     for group, ref in enumerate(messages):
         ref[ref.shape[0] - SUB :, :] = jnp.zeros((SUB, LANES), jnp.float32)
@@ -420,9 +458,10 @@
             vm(metric.shape, f32),
             vm(coriolis.shape, f32),
             vm(send.shape, jnp.int32),
-            vm((3, SUB * NODES, levels), f32),
+            vm((elements // SUB, 3, SUB * NODES, levels), f32),
             vm((plan.rows, rows), bf16),
-            vm((elements, LANES), f32),
+            vm((plan.rows, wide), f32),
+            vm((5, rows, LANES), f32),
             pltpu.SemaphoreType.DMA((5,)),
             pltpu.SemaphoreType.DMA((4,)),
         ),

time: 24.6 us -> 24.2 us (0.984)
  Pallas kernels: 6.81 us -> 6.45 us
    pallas_call x4, Pallas kernels: 6.81 us -> 6.45 us  [call(): pl.pallas_call(kernel, out_shape=[jax.ShapeDtypeStruct(shape, dtype) for...]
where the time goes in v1:
time: 24.2 us; the launch traced here: 24 us
  starting transfers between devices  14.4 us (60%)
  Pallas kernels  6.45 us (27%)
  waiting for transfers between devices  3.15 us (13%)
    ppermute x6, starting transfers between devices, shift(): lax.ppermute(value, AXES, [(d, (d + steps) % count) for d in range(count)])  14.4 us
    pallas_call x4, Pallas kernels, call(): pl.pallas_call(kernel, out_shape=[jax.ShapeDtypeStruct(shape, dtype) for...  6.45 us
    ppermute x6, waiting for transfers between devices, shift(): lax.ppermute(value, AXES, [(d, (d + steps) % count) for d in range(count)])  3.15 us
  transfers between devices with their start and end apart: 6, of which 2 were waited for; matrix products, arithmetic and copies ran while one was open for 0% of the time, Pallas kernels for 6%

profile of v1, /device:TPU:0, one launch (start us, length us, event | category | flops | bytes accessed | tf_op | source)
XLA Modules:
  0.0 24.0 jit_solution(2889217532408732901)
XLA Ops:
  0.0 3.6 %shard_map.64 = (bf16[3,64,16,128]{3,2,1,0:T(8,128)(2,1)S(1)}, bf16[1024,512]{1,0:T(8,128)(2,1)S(1)}, f32[8,128]{1,0:T(8,128)S(1)}, s32[16,64]{1,0:T(8,128)S(1)}...) custom-call(bf16[3,64,16,128]{3,2,1,0:T(8,128)(2,1)} %refs_0_.1, ...), custom_call_target="tpu_custom_call" | custom-call | tf_op jit(solution)/shard_map/pallas_call | solution.py:420
  3.6 3.1 %collective-permute-start.2 = (f32[296,128]{1,0:T(8,128)S(1)}, f32[296,128]{1,0:T(8,128)S(1)}, u32[]{:S(2)}, u32[]{:S(2)}) collective-permute-start(f32[296,128]{1,0:T(8,128)S(1)} %get-tuple-element.27), channel_id=1, source_target_pairs={{0,8},{1,9},{2,10},{3,11},{4,12},{5,13},{6,14},{7,15},{8,16},{9,17... | collective-permute-start | bytes 454664 | tf_op jit(solution)/shard_map/ppermute | solution.py:25
  6.7 2.1 %collective-permute-start.3 = (f32[296,128]{1,0:T(8,128)S(1)}, f32[296,128]{1,0:T(8,128)S(1)}, u32[]{:S(2)}, u32[]{:S(2)}) collective-permute-start(f32[296,128]{1,0:T(8,128)S(1)} %get-tuple-element.28), channel_id=1, source_target_pairs={{0,24},{1,25},{2,26},{3,27},{4,28},{5,29},{6,30},{7,31},{8,0},{9,1... | collective-permute-start | bytes 454664 | tf_op jit(solution)/shard_map/ppermute | solution.py:25
  8.8 1.7 %collective-permute-start = (f32[32,128]{1,0:T(8,128)S(1)}, f32[32,128]{1,0:T(8,128)S(1)}, u32[]{:S(2)}, u32[]{:S(2)}) collective-permute-start(f32[32,128]{1,0:T(8,128)S(1)} %get-tuple-element.25), channel_id=1, source_target_pairs={{0,1},{1,2},{2,3},{3,4},{4,5},{5,6},{6,7},{7,8},{8,9},{9,10},{10,1... | collective-permute-start | bytes 49160 | tf_op jit(solution)/shard_map/ppermute | solution.py:25
  10.5 3.7 %collective-permute-start.1 = (f32[32,128]{1,0:T(8,128)S(1)}, f32[32,128]{1,0:T(8,128)S(1)}, u32[]{:S(2)}, u32[]{:S(2)}) collective-permute-start(f32[32,128]{1,0:T(8,128)S(1)} %get-tuple-element.26), channel_id=1, source_target_pairs={{0,31},{1,0},{2,1},{3,2},{4,3},{5,4},{6,5},{7,6},{8,7},{9,8},{10,9... | collective-permute-start | bytes 49160 | tf_op jit(solution)/shard_map/ppermute | solution.py:25
  14.2 1.4 %shard_map.65 = (f32[1024,512]{1,0:T(8,128)S(1)}, bf16[1024,256]{1,0:T(8,128)(2,1)S(1)}) custom-call(bf16[1024,512]{1,0:T(8,128)(2,1)S(1)} %get-tuple-element.19.refs_0_, f32[8,128]{1,0:T(8,128)S(1)} %get-tuple-element.20.refs_1_, s32[16,64]{1,0:T(8,128)S(1)} %get-tuple-element.21.refs_2_, s32[1,212]{1,0:T(1,128)S(1)} %get-tuple-element.22.refs_3_), custom_call_target="tpu_custom_call" | custom-call | tf_op jit(solution)/shard_map/pallas_call | solution.py:420
  15.6 1.6 %collective-permute-done.refs_0_.refs_3_ = f32[32,128]{1,0:T(8,128)S(1)} collective-permute-done((f32[32,128]{1,0:T(8,128)S(1)}, f32[32,128]{1,0:T(8,128)S(1)}, u32[]{:S(2)}, u32[]{:S(2)}) %collective-permute-start) | collective-permute-done | bytes 16416 | tf_op jit(solution)/shard_map/ppermute | solution.py:25
  17.2 0.0 collective-permute-done.1.refs_1_.refs_4_
  17.2 0.1 collective-permute-start.4
  17.2 3.8 %collective-permute-start.5 = (f32[8,128]{1,0:T(8,128)S(1)}, f32[8,128]{1,0:T(8,128)S(1)}, u32[]{:S(2)}, u32[]{:S(2)}) collective-permute-start(f32[8,128]{1,0:T(8,128)S(1)} %get-tuple-element.30), channel_id=1, source_target_pairs={{0,24},{1,25},{2,26},{3,27},{4,28},{5,29},{6,30},{7,31},{8,0},{9,1... | collective-permute-start | bytes 12296 | tf_op jit(solution)/shard_map/ppermute | solution.py:25
  21.0 1.6 %collective-permute-done.4.refs_7_ = f32[8,128]{1,0:T(8,128)S(1)} collective-permute-done((f32[8,128]{1,0:T(8,128)S(1)}, f32[8,128]{1,0:T(8,128)S(1)}, u32[]{:S(2)}, u32[]{:S(2)}) %collective-permute-start.4) | collective-permute-done | bytes 4128 | tf_op jit(solution)/shard_map/ppermute | solution.py:25
  22.6 0.0 collective-permute-done.5.refs_8_
  22.6 0.0 collective-permute-done.2.refs_5_
  22.6 0.0 collective-permute-done.3.refs_6_
  22.6 1.4 %shard_map.67 = bf16[3,64,16,128]{3,2,1,0:T(8,128)(2,1)} custom-call(bf16[3,64,16,128]{3,2,1,0:T(8,128)(2,1)S(1)} %get-tuple-element.18.refs_0_, f32[1024,512]{1,0:T(8,128)S(1)} %get-tuple-element.23.refs_2_.refs_1_, bf16[1024,256]{1,0:T(8,128)(2,1)S(1)} %get-tuple-element.24.refs_2_, f32[32,128]{1,0:T(8,128)S(1)} %collective-permute-done.refs_0_.refs_3_, ...), custom_call_target="tpu_custom_call" | custom-call | tf_op jit(solution)/shard_map/pallas_call | solution.py:420
  (1 shorter events, 0.0 us)
Async XLA Ops:
  3.6 19.0 %collective-permute-start.2 = (f32[296,128]{1,0:T(8,128)S(1)}, f32[296,128]{1,0:T(8,128)S(1)}, u32[]{:S(2)}, u32[]{:S(2)}) collective-permute-start(f32[296,128]{1,0:T(8,128)S(1)} %get-tuple-element.27), channel_id=1, source_target_pairs={{0,8},{1,9},{2,10},{3,11},{4,12},{5,13},{6,14},{7,15},{8,16},{9,17... | collective-permute-start | bytes 454664 | tf_op jit(solution)/shard_map/ppermute | solution.py:25
  6.7 15.9 %collective-permute-start.3 = (f32[296,128]{1,0:T(8,128)S(1)}, f32[296,128]{1,0:T(8,128)S(1)}, u32[]{:S(2)}, u32[]{:S(2)}) collective-permute-start(f32[296,128]{1,0:T(8,128)S(1)} %get-tuple-element.28), channel_id=1, source_target_pairs={{0,24},{1,25},{2,26},{3,27},{4,28},{5,29},{6,30},{7,31},{8,0},{9,1... | collective-permute-start | bytes 454664 | tf_op jit(solution)/shard_map/ppermute | solution.py:25
  8.8 8.3 %collective-permute-start = (f32[32,128]{1,0:T(8,128)S(1)}, f32[32,128]{1,0:T(8,128)S(1)}, u32[]{:S(2)}, u32[]{:S(2)}) collective-permute-start(f32[32,128]{1,0:T(8,128)S(1)} %get-tuple-element.25), channel_id=1, source_target_pairs={{0,1},{1,2},{2,3},{3,4},{4,5},{5,6},{6,7},{7,8},{8,9},{9,10},{10,1... | collective-permute-start | bytes 49160 | tf_op jit(solution)/shard_map/ppermute | solution.py:25
  10.5 6.7 %collective-permute-start.1 = (f32[32,128]{1,0:T(8,128)S(1)}, f32[32,128]{1,0:T(8,128)S(1)}, u32[]{:S(2)}, u32[]{:S(2)}) collective-permute-start(f32[32,128]{1,0:T(8,128)S(1)} %get-tuple-element.26), channel_id=1, source_target_pairs={{0,31},{1,0},{2,1},{3,2},{4,3},{5,4},{6,5},{7,6},{8,7},{9,8},{10,9... | collective-permute-start | bytes 49160 | tf_op jit(solution)/shard_map/ppermute | solution.py:25
  17.2 5.5 %collective-permute-start.4 = (f32[8,128]{1,0:T(8,128)S(1)}, f32[8,128]{1,0:T(8,128)S(1)}, u32[]{:S(2)}, u32[]{:S(2)}) collective-permute-start(f32[8,128]{1,0:T(8,128)S(1)} %get-tuple-element.29), channel_id=1, source_target_pairs={{0,8},{1,9},{2,10},{3,11},{4,12},{5,13},{6,14},{7,15},{8,16},{9,17... | collective-permute-start | bytes 12296 | tf_op jit(solution)/shard_map/ppermute | solution.py:25
  17.2 5.4 %collective-permute-start.5 = (f32[8,128]{1,0:T(8,128)S(1)}, f32[8,128]{1,0:T(8,128)S(1)}, u32[]{:S(2)}, u32[]{:S(2)}) collective-permute-start(f32[8,128]{1,0:T(8,128)S(1)} %get-tuple-element.30), channel_id=1, source_target_pairs={{0,24},{1,25},{2,26},{3,27},{4,28},{5,29},{6,30},{7,31},{8,0},{9,1... | collective-permute-start | bytes 12296 | tf_op jit(solution)/shard_map/ppermute | solution.py:25

commit v2 on v1

--- a/solution.py
+++ b/solution.py
@@ -349,7 +349,7 @@
     local_sums(values, numbers, weighted, own)
 
 
-def relay_kernel(plan, left, right, own, up, down):
+def relay_kernel(plan, left, right, up, down):
     start = plan.weight_row(0)
     for i, ref in enumerate((up, down)):
         place = plan.blocks(0)[-2 + i][1]
@@ -477,10 +477,7 @@
         (weighted, numbers, points, recv),
     )
     relays = call(
-        lambda *refs: relay_kernel(plan, *refs),
-        (((SUB, LANES), f32, vm),) * 2,
-        (vm, vm, pl.ANY),
-        (landed[0], landed[1], own),
+        lambda *refs: relay_kernel(plan, *refs), (((SUB, LANES), f32, vm),) * 2, (vm, vm), (landed[0], landed[1])
     )
     passed = []
     for i, offset in enumerate((plan.lap, -plan.lap)):

time: 24.2 us -> 24.3 us (level)
  no operation moved by 1% of the time
where the time goes in v2:
time: 24.3 us; the launch traced here: 24.1 us
  starting transfers between devices  14.4 us (59%)
  Pallas kernels  6.49 us (27%)
  waiting for transfers between devices  3.14 us (13%)
    ppermute x6, starting transfers between devices, shift(): lax.ppermute(value, AXES, [(d, (d + steps) % count) for d in range(count)])  14.4 us
    pallas_call x4, Pallas kernels, call(): pl.pallas_call(kernel, out_shape=[jax.ShapeDtypeStruct(shape, dtype) for...  6.49 us
    ppermute x6, waiting for transfers between devices, shift(): lax.ppermute(value, AXES, [(d, (d + steps) % count) for d in range(count)])  3.14 us
  transfers between devices with their start and end apart: 6, of which 2 were waited for; matrix products, arithmetic and copies ran while one was open for 0% of the time, Pallas kernels for 6%

profile of v2, /device:TPU:0, one launch (start us, length us, event | category | flops | bytes accessed | tf_op | source)
XLA Modules:
  0.0 24.1 jit_solution(4364345940182078851)
XLA Ops:
  0.0 3.7 %shard_map.64 = (bf16[3,64,16,128]{3,2,1,0:T(8,128)(2,1)S(1)}, bf16[1024,512]{1,0:T(8,128)(2,1)S(1)}, f32[8,128]{1,0:T(8,128)S(1)}, s32[16,64]{1,0:T(8,128)S(1)}...) custom-call(bf16[3,64,16,128]{3,2,1,0:T(8,128)(2,1)} %refs_0_.1, ...), custom_call_target="tpu_custom_call" | custom-call | tf_op jit(solution)/shard_map/pallas_call | solution.py:420
  3.7 3.1 %collective-permute-start.2 = (f32[296,128]{1,0:T(8,128)S(1)}, f32[296,128]{1,0:T(8,128)S(1)}, u32[]{:S(2)}, u32[]{:S(2)}) collective-permute-start(f32[296,128]{1,0:T(8,128)S(1)} %get-tuple-element.27), channel_id=1, source_target_pairs={{0,8},{1,9},{2,10},{3,11},{4,12},{5,13},{6,14},{7,15},{8,16},{9,17... | collective-permute-start | bytes 454664 | tf_op jit(solution)/shard_map/ppermute | solution.py:25
  6.8 2.1 %collective-permute-start.3 = (f32[296,128]{1,0:T(8,128)S(1)}, f32[296,128]{1,0:T(8,128)S(1)}, u32[]{:S(2)}, u32[]{:S(2)}) collective-permute-start(f32[296,128]{1,0:T(8,128)S(1)} %get-tuple-element.28), channel_id=1, source_target_pairs={{0,24},{1,25},{2,26},{3,27},{4,28},{5,29},{6,30},{7,31},{8,0},{9,1... | collective-permute-start | bytes 454664 | tf_op jit(solution)/shard_map/ppermute | solution.py:25
  8.9 1.7 %collective-permute-start = (f32[32,128]{1,0:T(8,128)S(1)}, f32[32,128]{1,0:T(8,128)S(1)}, u32[]{:S(2)}, u32[]{:S(2)}) collective-permute-start(f32[32,128]{1,0:T(8,128)S(1)} %get-tuple-element.25), channel_id=1, source_target_pairs={{0,1},{1,2},{2,3},{3,4},{4,5},{5,6},{6,7},{7,8},{8,9},{9,10},{10,1... | collective-permute-start | bytes 49160 | tf_op jit(solution)/shard_map/ppermute | solution.py:25
  10.5 3.7 %collective-permute-start.1 = (f32[32,128]{1,0:T(8,128)S(1)}, f32[32,128]{1,0:T(8,128)S(1)}, u32[]{:S(2)}, u32[]{:S(2)}) collective-permute-start(f32[32,128]{1,0:T(8,128)S(1)} %get-tuple-element.26), channel_id=1, source_target_pairs={{0,31},{1,0},{2,1},{3,2},{4,3},{5,4},{6,5},{7,6},{8,7},{9,8},{10,9... | collective-permute-start | bytes 49160 | tf_op jit(solution)/shard_map/ppermute | solution.py:25
  14.2 3.0 %collective-permute-done.refs_0_.refs_3_ = f32[32,128]{1,0:T(8,128)S(1)} collective-permute-done((f32[32,128]{1,0:T(8,128)S(1)}, f32[32,128]{1,0:T(8,128)S(1)}, u32[]{:S(2)}, u32[]{:S(2)}) %collective-permute-start) | collective-permute-done | bytes 16416 | tf_op jit(solution)/shard_map/ppermute | solution.py:25
  17.2 0.0 collective-permute-done.1.refs_1_.refs_4_
  17.2 0.1 collective-permute-start.4
  17.2 3.8 %collective-permute-start.5 = (f32[8,128]{1,0:T(8,128)S(1)}, f32[8,128]{1,0:T(8,128)S(1)}, u32[]{:S(2)}, u32[]{:S(2)}) collective-permute-start(f32[8,128]{1,0:T(8,128)S(1)} %get-tuple-element.30), channel_id=1, source_target_pairs={{0,24},{1,25},{2,26},{3,27},{4,28},{5,29},{6,30},{7,31},{8,0},{9,1... | collective-permute-start | bytes 12296 | tf_op jit(solution)/shard_map/ppermute | solution.py:25
  21.1 1.4 %shard_map.65 = (f32[1024,512]{1,0:T(8,128)S(1)}, bf16[1024,256]{1,0:T(8,128)(2,1)S(1)}) custom-call(bf16[1024,512]{1,0:T(8,128)(2,1)S(1)} %get-tuple-element.19.refs_0_, f32[8,128]{1,0:T(8,128)S(1)} %get-tuple-element.20.refs_1_, s32[16,64]{1,0:T(8,128)S(1)} %get-tuple-element.21.refs_2_, s32[1,212]{1,0:T(1,128)S(1)} %get-tuple-element.22.refs_3_), custom_call_target="tpu_custom_call" | custom-call | tf_op jit(solution)/shard_map/pallas_call | solution.py:420
  22.5 0.2 collective-permute-done.4.refs_7_
  22.6 0.0 collective-permute-done.5.refs_8_
  22.6 0.0 collective-permute-done.2.refs_5_
  22.6 0.0 collective-permute-done.3.refs_6_
  22.6 1.4 %shard_map.67 = bf16[3,64,16,128]{3,2,1,0:T(8,128)(2,1)} custom-call(bf16[3,64,16,128]{3,2,1,0:T(8,128)(2,1)S(1)} %get-tuple-element.18.refs_0_, f32[1024,512]{1,0:T(8,128)S(1)} %get-tuple-element.23.refs_1_, bf16[1024,256]{1,0:T(8,128)(2,1)S(1)} %get-tuple-element.24.refs_2_, f32[32,128]{1,0:T(8,128)S(1)} %collective-permute-done.refs_0_.refs_3_, ...), custom_call_target="tpu_custom_call" | custom-call | tf_op jit(solution)/shard_map/pallas_call | solution.py:420
  (1 shorter events, 0.0 us)
Async XLA Ops:
  3.7 19.0 %collective-permute-start.2 = (f32[296,128]{1,0:T(8,128)S(1)}, f32[296,128]{1,0:T(8,128)S(1)}, u32[]{:S(2)}, u32[]{:S(2)}) collective-permute-start(f32[296,128]{1,0:T(8,128)S(1)} %get-tuple-element.27), channel_id=1, source_target_pairs={{0,8},{1,9},{2,10},{3,11},{4,12},{5,13},{6,14},{7,15},{8,16},{9,17... | collective-permute-start | bytes 454664 | tf_op jit(solution)/shard_map/ppermute | solution.py:25
  6.8 15.9 %collective-permute-start.3 = (f32[296,128]{1,0:T(8,128)S(1)}, f32[296,128]{1,0:T(8,128)S(1)}, u32[]{:S(2)}, u32[]{:S(2)}) collective-permute-start(f32[296,128]{1,0:T(8,128)S(1)} %get-tuple-element.28), channel_id=1, source_target_pairs={{0,24},{1,25},{2,26},{3,27},{4,28},{5,29},{6,30},{7,31},{8,0},{9,1... | collective-permute-start | bytes 454664 | tf_op jit(solution)/shard_map/ppermute | solution.py:25
  8.9 8.3 %collective-permute-start = (f32[32,128]{1,0:T(8,128)S(1)}, f32[32,128]{1,0:T(8,128)S(1)}, u32[]{:S(2)}, u32[]{:S(2)}) collective-permute-start(f32[32,128]{1,0:T(8,128)S(1)} %get-tuple-element.25), channel_id=1, source_target_pairs={{0,1},{1,2},{2,3},{3,4},{4,5},{5,6},{6,7},{7,8},{8,9},{9,10},{10,1... | collective-permute-start | bytes 49160 | tf_op jit(solution)/shard_map/ppermute | solution.py:25
  10.5 6.7 %collective-permute-start.1 = (f32[32,128]{1,0:T(8,128)S(1)}, f32[32,128]{1,0:T(8,128)S(1)}, u32[]{:S(2)}, u32[]{:S(2)}) collective-permute-start(f32[32,128]{1,0:T(8,128)S(1)} %get-tuple-element.26), channel_id=1, source_target_pairs={{0,31},{1,0},{2,1},{3,2},{4,3},{5,4},{6,5},{7,6},{8,7},{9,8},{10,9... | collective-permute-start | bytes 49160 | tf_op jit(solution)/shard_map/ppermute | solution.py:25
  17.2 5.5 %collective-permute-start.4 = (f32[8,128]{1,0:T(8,128)S(1)}, f32[8,128]{1,0:T(8,128)S(1)}, u32[]{:S(2)}, u32[]{:S(2)}) collective-permute-start(f32[8,128]{1,0:T(8,128)S(1)} %get-tuple-element.29), channel_id=1, source_target_pairs={{0,8},{1,9},{2,10},{3,11},{4,12},{5,13},{6,14},{7,15},{8,16},{9,17... | collective-permute-start | bytes 12296 | tf_op jit(solution)/shard_map/ppermute | solution.py:25
  17.2 5.4 %collective-permute-start.5 = (f32[8,128]{1,0:T(8,128)S(1)}, f32[8,128]{1,0:T(8,128)S(1)}, u32[]{:S(2)}, u32[]{:S(2)}) collective-permute-start(f32[8,128]{1,0:T(8,128)S(1)} %get-tuple-element.30), channel_id=1, source_target_pairs={{0,24},{1,25},{2,26},{3,27},{4,28},{5,29},{6,30},{7,31},{8,0},{9,1... | collective-permute-start | bytes 12296 | tf_op jit(solution)/shard_map/ppermute | solution.py:25

commit v3 on v2

--- a/solution.py
+++ b/solution.py
@@ -194,13 +194,12 @@
         )
         for i in range(chunks)
     ]
-    larges[0].start()
+    for copy in larges:
+        copy.start()
     later = pltpu.make_async_copy(recv, recv_v, sems.at[4])
     later.start()
     for copy in smalls:
         copy.wait()
-    for copy in larges[1:]:
-        copy.start()
     rows = plan.rows
     wanted = as_column(arranged(send_v, plan), rows)
     _, scale = gll_tables()
@@ -217,6 +216,7 @@
     stack = (a * inv, b * inv, e * inv, g * inv, mass * cor_v[...], upper, mass - upper, pts_v[...].astype(jnp.float32))
     stack = jnp.transpose(jnp.concatenate(stack, axis=0))
     numbers[...] = point_rows(stack, 7 * NODES)
+    step = groups // chunks
     square = (LANES, LANES)
     kind = iota(square, 0) // NODES
     half = (iota(square, 1) >= LANES // 2).astype(jnp.int32)
@@ -225,20 +225,24 @@
     lift = jnp.concatenate([jnp.concatenate(lift + [(kind == 5 + half).astype(jnp.bfloat16)], axis=1), fine], axis=0)
     coarse = stack.astype(jnp.bfloat16).astype(jnp.float32)
     slot = iota((SUB, LANES), 1) % NODES
-    for group in range(groups):
-        here = slice(group * SUB, (group + 1) * SUB)
-        picked = jnp.concatenate(
-            [
-                jnp.concatenate([jnp.where(slot == k, part[here], 0.0) for k in range(NODES)], axis=0)
-                for part in (coarse, stack - coarse)
-            ],
-            axis=1,
-        ).astype(jnp.bfloat16)
-        there = slice(group * LANES, (group + 1) * LANES)
-        wide = jnp.dot(picked, lift, preferred_element_type=jnp.float32)
-        for i in range(5):
-            coefs[i, there, :] = wide[:, i * LANES : (i + 1) * LANES]
-        weighted[there, MASS:] = wide[:, 5 * LANES :].astype(jnp.bfloat16)
+
+    def lifted(i):
+        for group in range(i * step, (i + 1) * step):
+            here = slice(group * SUB, (group + 1) * SUB)
+            picked = jnp.concatenate(
+                [
+                    jnp.concatenate([jnp.where(slot == k, part[here], 0.0) for k in range(NODES)], axis=0)
+                    for part in (coarse, stack - coarse)
+                ],
+                axis=1,
+            ).astype(jnp.bfloat16)
+            there = slice(group * LANES, (group + 1) * LANES)
+            wide = jnp.dot(picked, lift, preferred_element_type=jnp.float32)
+            for which in range(5):
+                coefs[which, there, :] = wide[:, which * LANES : (which + 1) * LANES]
+            weighted[there, MASS:] = wide[:, 5 * LANES :].astype(jnp.bfloat16)
+
+    lifted(0)
     for group in range(groups):
         mask[:, group * LANES : (group + 1) * LANES] = (
             jnp.broadcast_to(wanted, (rows, LANES)) == numbers[group : group + 1, :]
@@ -270,13 +274,11 @@
         for f, part in enumerate(parts):
             weighted[there, f * LANES : (f + 1) * LANES] = jnp.concatenate(part, axis=0).astype(jnp.bfloat16)
 
-    step = groups // chunks
     turn = (
         iota(square, 1) == iota(square, 0) % SUB * NODES + iota(square, 0) // SUB
     ).astype(jnp.bfloat16)
 
     def reorder(i):
-        larges[i].wait()
         for group in range(i * step, (i + 1) * step):
             here = slice(group * SUB, (group + 1) * SUB)
             for f in range(3):
@@ -289,14 +291,17 @@
         part = jnp.dot(mask[:, span], weighted[span, :], preferred_element_type=jnp.float32)
         total[...] = part if i == 0 else total[...] + part
 
+    for copy in larges:
+        copy.wait()
     reorder(0)
     for i in range(chunks):
-        if i + 1 < chunks:
-            reorder(i + 1)
         for group in range(i * step, (i + 1) * step):
             body(group)
         if i:
             gather(i - 1)
+        if i + 1 < chunks:
+            reorder(i + 1)
+            lifted(i + 1)
     gather(chunks - 1)
     later.wait()
     sums = total[...]

time: 24.3 us -> 24 us (0.988)
  Pallas kernels: 6.49 us -> 6.23 us
    pallas_call x4, Pallas kernels: 6.49 us -> 6.23 us  [call(): pl.pallas_call(kernel, out_shape=[jax.ShapeDtypeStruct(shape, dtype) for...]
where the time goes in v3:
time: 24 us; the launch traced here: 23.8 us
  starting transfers between devices  14.4 us (60%)
  Pallas kernels  6.23 us (26%)
  waiting for transfers between devices  3.14 us (13%)
    ppermute x6, starting transfers between devices, shift(): lax.ppermute(value, AXES, [(d, (d + steps) % count) for d in range(count)])  14.4 us
    pallas_call x4, Pallas kernels, call(): pl.pallas_call(kernel, out_shape=[jax.ShapeDtypeStruct(shape, dtype) for...  6.23 us
    ppermute x6, waiting for transfers between devices, shift(): lax.ppermute(value, AXES, [(d, (d + steps) % count) for d in range(count)])  3.14 us
  transfers between devices with their start and end apart: 6, of which 2 were waited for; matrix products, arithmetic and copies ran while one was open for 0% of the time, Pallas kernels for 6%

profile of v3, /device:TPU:0, one launch (start us, length us, event | category | flops | bytes accessed | tf_op | source)
XLA Modules:
  0.0 23.8 jit_solution(1071616849323232853)
XLA Ops:
  0.0 3.4 %shard_map.64 = (bf16[3,64,16,128]{3,2,1,0:T(8,128)(2,1)S(1)}, bf16[1024,512]{1,0:T(8,128)(2,1)S(1)}, f32[8,128]{1,0:T(8,128)S(1)}, s32[16,64]{1,0:T(8,128)S(1)}...) custom-call(bf16[3,64,16,128]{3,2,1,0:T(8,128)(2,1)} %refs_0_.1, ...), custom_call_target="tpu_custom_call" | custom-call | tf_op jit(solution)/shard_map/pallas_call | solution.py:425
  3.4 3.1 %collective-permute-start.2 = (f32[296,128]{1,0:T(8,128)S(1)}, f32[296,128]{1,0:T(8,128)S(1)}, u32[]{:S(2)}, u32[]{:S(2)}) collective-permute-start(f32[296,128]{1,0:T(8,128)S(1)} %get-tuple-element.27), channel_id=1, source_target_pairs={{0,8},{1,9},{2,10},{3,11},{4,12},{5,13},{6,14},{7,15},{8,16},{9,17... | collective-permute-start | bytes 454664 | tf_op jit(solution)/shard_map/ppermute | solution.py:25
  6.5 2.1 %collective-permute-start.3 = (f32[296,128]{1,0:T(8,128)S(1)}, f32[296,128]{1,0:T(8,128)S(1)}, u32[]{:S(2)}, u32[]{:S(2)}) collective-permute-start(f32[296,128]{1,0:T(8,128)S(1)} %get-tuple-element.28), channel_id=1, source_target_pairs={{0,24},{1,25},{2,26},{3,27},{4,28},{5,29},{6,30},{7,31},{8,0},{9,1... | collective-permute-start | bytes 454664 | tf_op jit(solution)/shard_map/ppermute | solution.py:25
  8.6 1.6 %collective-permute-start = (f32[32,128]{1,0:T(8,128)S(1)}, f32[32,128]{1,0:T(8,128)S(1)}, u32[]{:S(2)}, u32[]{:S(2)}) collective-permute-start(f32[32,128]{1,0:T(8,128)S(1)} %get-tuple-element.25), channel_id=1, source_target_pairs={{0,1},{1,2},{2,3},{3,4},{4,5},{5,6},{6,7},{7,8},{8,9},{9,10},{10,1... | collective-permute-start | bytes 49160 | tf_op jit(solution)/shard_map/ppermute | solution.py:25
  10.2 3.7 %collective-permute-start.1 = (f32[32,128]{1,0:T(8,128)S(1)}, f32[32,128]{1,0:T(8,128)S(1)}, u32[]{:S(2)}, u32[]{:S(2)}) collective-permute-start(f32[32,128]{1,0:T(8,128)S(1)} %get-tuple-element.26), channel_id=1, source_target_pairs={{0,31},{1,0},{2,1},{3,2},{4,3},{5,4},{6,5},{7,6},{8,7},{9,8},{10,9... | collective-permute-start | bytes 49160 | tf_op jit(solution)/shard_map/ppermute | solution.py:25
  13.9 3.0 %collective-permute-done.refs_0_.refs_3_ = f32[32,128]{1,0:T(8,128)S(1)} collective-permute-done((f32[32,128]{1,0:T(8,128)S(1)}, f32[32,128]{1,0:T(8,128)S(1)}, u32[]{:S(2)}, u32[]{:S(2)}) %collective-permute-start) | collective-permute-done | bytes 16416 | tf_op jit(solution)/shard_map/ppermute | solution.py:25
  16.9 0.0 collective-permute-done.1.refs_1_.refs_4_
  16.9 0.1 collective-permute-start.4
  17.0 3.8 %collective-permute-start.5 = (f32[8,128]{1,0:T(8,128)S(1)}, f32[8,128]{1,0:T(8,128)S(1)}, u32[]{:S(2)}, u32[]{:S(2)}) collective-permute-start(f32[8,128]{1,0:T(8,128)S(1)} %get-tuple-element.30), channel_id=1, source_target_pairs={{0,24},{1,25},{2,26},{3,27},{4,28},{5,29},{6,30},{7,31},{8,0},{9,1... | collective-permute-start | bytes 12296 | tf_op jit(solution)/shard_map/ppermute | solution.py:25
  20.8 1.4 %shard_map.65 = (f32[1024,512]{1,0:T(8,128)S(1)}, bf16[1024,256]{1,0:T(8,128)(2,1)S(1)}) custom-call(bf16[1024,512]{1,0:T(8,128)(2,1)S(1)} %get-tuple-element.19.refs_0_, f32[8,128]{1,0:T(8,128)S(1)} %get-tuple-element.20.refs_1_, s32[16,64]{1,0:T(8,128)S(1)} %get-tuple-element.21.refs_2_, s32[1,212]{1,0:T(1,128)S(1)} %get-tuple-element.22.refs_3_), custom_call_target="tpu_custom_call" | custom-call | tf_op jit(solution)/shard_map/pallas_call | solution.py:425
  22.2 0.2 collective-permute-done.4.refs_7_
  22.4 0.0 collective-permute-done.5.refs_8_
  22.4 0.0 collective-permute-done.2.refs_5_
  22.4 0.0 collective-permute-done.3.refs_6_
  22.4 1.4 %shard_map.67 = bf16[3,64,16,128]{3,2,1,0:T(8,128)(2,1)} custom-call(bf16[3,64,16,128]{3,2,1,0:T(8,128)(2,1)S(1)} %get-tuple-element.18.refs_0_, f32[1024,512]{1,0:T(8,128)S(1)} %get-tuple-element.23.refs_1_, bf16[1024,256]{1,0:T(8,128)(2,1)S(1)} %get-tuple-element.24.refs_2_, f32[32,128]{1,0:T(8,128)S(1)} %collective-permute-done.refs_0_.refs_3_, ...), custom_call_target="tpu_custom_call" | custom-call | tf_op jit(solution)/shard_map/pallas_call | solution.py:425
  (1 shorter events, 0.0 us)
Async XLA Ops:
  3.4 19.0 %collective-permute-start.2 = (f32[296,128]{1,0:T(8,128)S(1)}, f32[296,128]{1,0:T(8,128)S(1)}, u32[]{:S(2)}, u32[]{:S(2)}) collective-permute-start(f32[296,128]{1,0:T(8,128)S(1)} %get-tuple-element.27), channel_id=1, source_target_pairs={{0,8},{1,9},{2,10},{3,11},{4,12},{5,13},{6,14},{7,15},{8,16},{9,17... | collective-permute-start | bytes 454664 | tf_op jit(solution)/shard_map/ppermute | solution.py:25
  6.5 15.9 %collective-permute-start.3 = (f32[296,128]{1,0:T(8,128)S(1)}, f32[296,128]{1,0:T(8,128)S(1)}, u32[]{:S(2)}, u32[]{:S(2)}) collective-permute-start(f32[296,128]{1,0:T(8,128)S(1)} %get-tuple-element.28), channel_id=1, source_target_pairs={{0,24},{1,25},{2,26},{3,27},{4,28},{5,29},{6,30},{7,31},{8,0},{9,1... | collective-permute-start | bytes 454664 | tf_op jit(solution)/shard_map/ppermute | solution.py:25
  8.6 8.3 %collective-permute-start = (f32[32,128]{1,0:T(8,128)S(1)}, f32[32,128]{1,0:T(8,128)S(1)}, u32[]{:S(2)}, u32[]{:S(2)}) collective-permute-start(f32[32,128]{1,0:T(8,128)S(1)} %get-tuple-element.25), channel_id=1, source_target_pairs={{0,1},{1,2},{2,3},{3,4},{4,5},{5,6},{6,7},{7,8},{8,9},{9,10},{10,1... | collective-permute-start | bytes 49160 | tf_op jit(solution)/shard_map/ppermute | solution.py:25
  10.2 6.7 %collective-permute-start.1 = (f32[32,128]{1,0:T(8,128)S(1)}, f32[32,128]{1,0:T(8,128)S(1)}, u32[]{:S(2)}, u32[]{:S(2)}) collective-permute-start(f32[32,128]{1,0:T(8,128)S(1)} %get-tuple-element.26), channel_id=1, source_target_pairs={{0,31},{1,0},{2,1},{3,2},{4,3},{5,4},{6,5},{7,6},{8,7},{9,8},{10,9... | collective-permute-start | bytes 49160 | tf_op jit(solution)/shard_map/ppermute | solution.py:25
  16.9 5.5 %collective-permute-start.4 = (f32[8,128]{1,0:T(8,128)S(1)}, f32[8,128]{1,0:T(8,128)S(1)}, u32[]{:S(2)}, u32[]{:S(2)}) collective-permute-start(f32[8,128]{1,0:T(8,128)S(1)} %get-tuple-element.29), channel_id=1, source_target_pairs={{0,8},{1,9},{2,10},{3,11},{4,12},{5,13},{6,14},{7,15},{8,16},{9,17... | collective-permute-start | bytes 12296 | tf_op jit(solution)/shard_map/ppermute | solution.py:25
  17.0 5.4 %collective-permute-start.5 = (f32[8,128]{1,0:T(8,128)S(1)}, f32[8,128]{1,0:T(8,128)S(1)}, u32[]{:S(2)}, u32[]{:S(2)}) collective-permute-start(f32[8,128]{1,0:T(8,128)S(1)} %get-tuple-element.30), channel_id=1, source_target_pairs={{0,24},{1,25},{2,26},{3,27},{4,28},{5,29},{6,30},{7,31},{8,0},{9,1... | collective-permute-start | bytes 12296 | tf_op jit(solution)/shard_map/ppermute | solution.py:25

commit v4 on v3

--- a/solution.py
+++ b/solution.py
@@ -180,8 +180,9 @@
     met_v, cor_v, send_v, tile, mask, total, coefs, sems, chunk_sems = refs[15:]
     elements = fields.shape[1]
     groups = elements // SUB
-    chunks = chunk_sems.shape[0]
-    per = elements // chunks
+    chunks = 4
+    cuts = chunk_sems.shape[0]
+    per = elements // cuts
     smalls = [
         pltpu.make_async_copy(source, target, sems.at[i])
         for i, (source, target) in enumerate(((points, pts_v), (send, send_v), (metric, met_v), (cor, cor_v)))
@@ -192,7 +193,7 @@
         pltpu.make_async_copy(
             prog.at[:, pl.ds(i * per, per)], fields.at[:, pl.ds(i * per, per)], chunk_sems.at[i]
         )
-        for i in range(chunks)
+        for i in range(cuts)
     ]
     for copy in larges:
         copy.start()
@@ -212,8 +213,9 @@
     )
     inv = 1.0 / (a * g - b * e)
     mass = quad * inv
-    upper = mass.astype(jnp.bfloat16).astype(jnp.float32)
-    stack = (a * inv, b * inv, e * inv, g * inv, mass * cor_v[...], upper, mass - upper, pts_v[...].astype(jnp.float32))
+    share = mass * np.float32(1.0 / STEP_SIZE)
+    upper = share.astype(jnp.bfloat16).astype(jnp.float32)
+    stack = (a * inv, b * inv, e * inv, g * inv, mass * cor_v[...], upper, share - upper, pts_v[...].astype(jnp.float32))
     stack = jnp.transpose(jnp.concatenate(stack, axis=0))
     numbers[...] = point_rows(stack, 7 * NODES)
     step = groups // chunks
@@ -255,16 +257,16 @@
         )
         u, v, h = ([tile[group, f, k * SUB : (k + 1) * SUB, :] for k in range(NODES)] for f in range(3))
         span = range(NODES)
-        energy = [0.5 * (u[k] * u[k] + v[k] * v[k]) + h[k] for k in span]
-        along = derive(energy, 1, scale, -1.0)
-        across = derive(energy, 0, scale, -1.0)
+        energy = [u[k] * u[k] + v[k] * v[k] + h[k] for k in span]
+        along = derive(energy, 1, scale, -0.5)
+        across = derive(energy, 0, scale, -0.5)
         grad_one = [ca[k] * along[k] + ce[k] * across[k] for k in span]
         grad_two = [cb[k] * along[k] + cg[k] * across[k] for k in span]
         turn_two = derive([ca[k] * v[k] - cb[k] * u[k] for k in span], 1, scale)
         turn_one = derive([cg[k] * u[k] - ce[k] * v[k] for k in span], 0, scale)
         eta = [turn_two[k] - turn_one[k] + cf[k] for k in span]
-        flow_one = derive([h[k] * (ca[k] * u[k] + cb[k] * v[k]) for k in span], 1, scale, -1.0)
-        flow_two = derive([h[k] * (ce[k] * u[k] + cg[k] * v[k]) for k in span], 0, scale, -1.0)
+        flow_one = derive([h[k] * (ca[k] * u[k] + cb[k] * v[k]) for k in span], 1, scale, -0.5)
+        flow_two = derive([h[k] * (ce[k] * u[k] + cg[k] * v[k]) for k in span], 0, scale, -0.5)
         parts = (
             [eta[k] * v[k] + grad_one[k] for k in span],
             [grad_two[k] - eta[k] * u[k] for k in span],
@@ -283,13 +285,13 @@
             here = slice(group * SUB, (group + 1) * SUB)
             for f in range(3):
                 tile[group, f] = jnp.dot(
-                    turn, fields[f, here].reshape(SUB * NODES, LANES), preferred_element_type=jnp.float32
+                    turn if f < 2 else 2.0 * turn, fields[f, here].reshape(SUB * NODES, LANES), preferred_element_type=jnp.float32
                 )
 
     def gather(i):
         span = slice(i * step * LANES, (i + 1) * step * LANES)
         part = jnp.dot(mask[:, span], weighted[span, :], preferred_element_type=jnp.float32)
-        total[...] = part if i == 0 else total[...] + part
+        return part if i == 0 else total[...] + part
 
     for copy in larges:
         copy.wait()
@@ -298,13 +300,12 @@
         for group in range(i * step, (i + 1) * step):
             body(group)
         if i:
-            gather(i - 1)
+            total[...] = gather(i - 1)
         if i + 1 < chunks:
             reorder(i + 1)
             lifted(i + 1)
-    gather(chunks - 1)
     later.wait()
-    sums = total[...]
+    sums = gather(chunks - 1)
     masses = as_row(both_halves(sums[:, MASS:]), plan.width)
     for group, ref in enumerate(messages):
         ref[ref.shape[0] - SUB :, :] = jnp.zeros((SUB, LANES), jnp.float32)
@@ -404,7 +405,7 @@
         rows = slice(i * per * NODES, (i + 1) * per * NODES)
         here = slice(i * per, (i + 1) * per)
         total = own[rows, :] + jnp.dot(table[rows, :], arrived, preferred_element_type=jnp.float32)
-        factor = np.float32(STEP_SIZE) / both_halves(total[:, MASS:])
+        factor = 1.0 / both_halves(total[:, MASS:])
         for f in range(3):
             moved = (total[:, f * LANES : (f + 1) * LANES] * factor).reshape(per, NODES, LANES)
             held[f, here] = (fields[f, here].astype(jnp.float32) + moved).astype(jnp.bfloat16)
@@ -468,7 +469,7 @@
             vm((plan.rows, wide), f32),
             vm((5, rows, LANES), f32),
             pltpu.SemaphoreType.DMA((5,)),
-            pltpu.SemaphoreType.DMA((4,)),
+            pltpu.SemaphoreType.DMA((1,)),
         ),
     )
     fields, weighted, numbers, points, recv = sent[:5]

time: 24 us -> 23.8 us (level)
  no operation moved by 1% of the time
where the time goes in v4:
time: 23.8 us; the launch traced here: 23.6 us
  starting transfers between devices  14.4 us (61%)
  Pallas kernels  6.02 us (25%)
  waiting for transfers between devices  3.17 us (13%)
    ppermute x6, starting transfers between devices, shift(): lax.ppermute(value, AXES, [(d, (d + steps) % count) for d in range(count)])  14.4 us
    pallas_call x4, Pallas kernels, call(): pl.pallas_call(kernel, out_shape=[jax.ShapeDtypeStruct(shape, dtype) for...  6.02 us
    ppermute x6, waiting for transfers between devices, shift(): lax.ppermute(value, AXES, [(d, (d + steps) % count) for d in range(count)])  3.17 us
  transfers between devices with their start and end apart: 6, of which 2 were waited for; matrix products, arithmetic and copies ran while one was open for 0% of the time, Pallas kernels for 6%

profile of v4, /device:TPU:0, one launch (start us, length us, event | category | flops | bytes accessed | tf_op | source)
XLA Modules:
  0.0 23.6 jit_solution(6758198042197376674)
XLA Ops:
  0.0 3.2 %shard_map.64 = (bf16[3,64,16,128]{3,2,1,0:T(8,128)(2,1)S(1)}, bf16[1024,512]{1,0:T(8,128)(2,1)S(1)}, f32[8,128]{1,0:T(8,128)S(1)}, s32[16,64]{1,0:T(8,128)S(1)}...) custom-call(bf16[3,64,16,128]{3,2,1,0:T(8,128)(2,1)} %refs_0_.1, ...), custom_call_target="tpu_custom_call" | custom-call | tf_op jit(solution)/shard_map/pallas_call | solution.py:426
  3.2 3.1 %collective-permute-start.2 = (f32[296,128]{1,0:T(8,128)S(1)}, f32[296,128]{1,0:T(8,128)S(1)}, u32[]{:S(2)}, u32[]{:S(2)}) collective-permute-start(f32[296,128]{1,0:T(8,128)S(1)} %get-tuple-element.27), channel_id=1, source_target_pairs={{0,8},{1,9},{2,10},{3,11},{4,12},{5,13},{6,14},{7,15},{8,16},{9,17... | collective-permute-start | bytes 454664 | tf_op jit(solution)/shard_map/ppermute | solution.py:25
  6.3 2.1 %collective-permute-start.3 = (f32[296,128]{1,0:T(8,128)S(1)}, f32[296,128]{1,0:T(8,128)S(1)}, u32[]{:S(2)}, u32[]{:S(2)}) collective-permute-start(f32[296,128]{1,0:T(8,128)S(1)} %get-tuple-element.28), channel_id=1, source_target_pairs={{0,24},{1,25},{2,26},{3,27},{4,28},{5,29},{6,30},{7,31},{8,0},{9,1... | collective-permute-start | bytes 454664 | tf_op jit(solution)/shard_map/ppermute | solution.py:25
  8.4 1.6 %collective-permute-start = (f32[32,128]{1,0:T(8,128)S(1)}, f32[32,128]{1,0:T(8,128)S(1)}, u32[]{:S(2)}, u32[]{:S(2)}) collective-permute-start(f32[32,128]{1,0:T(8,128)S(1)} %get-tuple-element.25), channel_id=1, source_target_pairs={{0,1},{1,2},{2,3},{3,4},{4,5},{5,6},{6,7},{7,8},{8,9},{9,10},{10,1... | collective-permute-start | bytes 49160 | tf_op jit(solution)/shard_map/ppermute | solution.py:25
  10.1 3.7 %collective-permute-start.1 = (f32[32,128]{1,0:T(8,128)S(1)}, f32[32,128]{1,0:T(8,128)S(1)}, u32[]{:S(2)}, u32[]{:S(2)}) collective-permute-start(f32[32,128]{1,0:T(8,128)S(1)} %get-tuple-element.26), channel_id=1, source_target_pairs={{0,31},{1,0},{2,1},{3,2},{4,3},{5,4},{6,5},{7,6},{8,7},{9,8},{10,9... | collective-permute-start | bytes 49160 | tf_op jit(solution)/shard_map/ppermute | solution.py:25
  13.8 3.0 %collective-permute-done.refs_0_.refs_3_ = f32[32,128]{1,0:T(8,128)S(1)} collective-permute-done((f32[32,128]{1,0:T(8,128)S(1)}, f32[32,128]{1,0:T(8,128)S(1)}, u32[]{:S(2)}, u32[]{:S(2)}) %collective-permute-start) | collective-permute-done | bytes 16416 | tf_op jit(solution)/shard_map/ppermute | solution.py:25
  16.8 0.0 collective-permute-done.1.refs_1_.refs_4_
  16.8 0.1 collective-permute-start.4
  16.8 3.8 %collective-permute-start.5 = (f32[8,128]{1,0:T(8,128)S(1)}, f32[8,128]{1,0:T(8,128)S(1)}, u32[]{:S(2)}, u32[]{:S(2)}) collective-permute-start(f32[8,128]{1,0:T(8,128)S(1)} %get-tuple-element.30), channel_id=1, source_target_pairs={{0,24},{1,25},{2,26},{3,27},{4,28},{5,29},{6,30},{7,31},{8,0},{9,1... | collective-permute-start | bytes 12296 | tf_op jit(solution)/shard_map/ppermute | solution.py:25
  20.7 1.4 %shard_map.65 = (f32[1024,512]{1,0:T(8,128)S(1)}, bf16[1024,256]{1,0:T(8,128)(2,1)S(1)}) custom-call(bf16[1024,512]{1,0:T(8,128)(2,1)S(1)} %get-tuple-element.19.refs_0_, f32[8,128]{1,0:T(8,128)S(1)} %get-tuple-element.20.refs_1_, s32[16,64]{1,0:T(8,128)S(1)} %get-tuple-element.21.refs_2_, s32[1,212]{1,0:T(1,128)S(1)} %get-tuple-element.22.refs_3_), custom_call_target="tpu_custom_call" | custom-call | tf_op jit(solution)/shard_map/pallas_call | solution.py:426
  22.1 0.2 collective-permute-done.4.refs_7_
  22.2 0.0 collective-permute-done.5.refs_8_
  22.2 0.0 collective-permute-done.2.refs_5_
  22.2 0.0 collective-permute-done.3.refs_6_
  22.2 1.4 %shard_map.67 = bf16[3,64,16,128]{3,2,1,0:T(8,128)(2,1)} custom-call(bf16[3,64,16,128]{3,2,1,0:T(8,128)(2,1)S(1)} %get-tuple-element.18.refs_0_, f32[1024,512]{1,0:T(8,128)S(1)} %get-tuple-element.23.refs_1_, bf16[1024,256]{1,0:T(8,128)(2,1)S(1)} %get-tuple-element.24.refs_2_, f32[32,128]{1,0:T(8,128)S(1)} %collective-permute-done.refs_0_.refs_3_, ...), custom_call_target="tpu_custom_call" | custom-call | tf_op jit(solution)/shard_map/pallas_call | solution.py:426
  (1 shorter events, 0.0 us)
Async XLA Ops:
  3.2 19.0 %collective-permute-start.2 = (f32[296,128]{1,0:T(8,128)S(1)}, f32[296,128]{1,0:T(8,128)S(1)}, u32[]{:S(2)}, u32[]{:S(2)}) collective-permute-start(f32[296,128]{1,0:T(8,128)S(1)} %get-tuple-element.27), channel_id=1, source_target_pairs={{0,8},{1,9},{2,10},{3,11},{4,12},{5,13},{6,14},{7,15},{8,16},{9,17... | collective-permute-start | bytes 454664 | tf_op jit(solution)/shard_map/ppermute | solution.py:25
  6.3 15.9 %collective-permute-start.3 = (f32[296,128]{1,0:T(8,128)S(1)}, f32[296,128]{1,0:T(8,128)S(1)}, u32[]{:S(2)}, u32[]{:S(2)}) collective-permute-start(f32[296,128]{1,0:T(8,128)S(1)} %get-tuple-element.28), channel_id=1, source_target_pairs={{0,24},{1,25},{2,26},{3,27},{4,28},{5,29},{6,30},{7,31},{8,0},{9,1... | collective-permute-start | bytes 454664 | tf_op jit(solution)/shard_map/ppermute | solution.py:25
  8.4 8.3 %collective-permute-start = (f32[32,128]{1,0:T(8,128)S(1)}, f32[32,128]{1,0:T(8,128)S(1)}, u32[]{:S(2)}, u32[]{:S(2)}) collective-permute-start(f32[32,128]{1,0:T(8,128)S(1)} %get-tuple-element.25), channel_id=1, source_target_pairs={{0,1},{1,2},{2,3},{3,4},{4,5},{5,6},{6,7},{7,8},{8,9},{9,10},{10,1... | collective-permute-start | bytes 49160 | tf_op jit(solution)/shard_map/ppermute | solution.py:25
  10.1 6.7 %collective-permute-start.1 = (f32[32,128]{1,0:T(8,128)S(1)}, f32[32,128]{1,0:T(8,128)S(1)}, u32[]{:S(2)}, u32[]{:S(2)}) collective-permute-start(f32[32,128]{1,0:T(8,128)S(1)} %get-tuple-element.26), channel_id=1, source_target_pairs={{0,31},{1,0},{2,1},{3,2},{4,3},{5,4},{6,5},{7,6},{8,7},{9,8},{10,9... | collective-permute-start | bytes 49160 | tf_op jit(solution)/shard_map/ppermute | solution.py:25
  16.8 5.5 %collective-permute-start.4 = (f32[8,128]{1,0:T(8,128)S(1)}, f32[8,128]{1,0:T(8,128)S(1)}, u32[]{:S(2)}, u32[]{:S(2)}) collective-permute-start(f32[8,128]{1,0:T(8,128)S(1)} %get-tuple-element.29), channel_id=1, source_target_pairs={{0,8},{1,9},{2,10},{3,11},{4,12},{5,13},{6,14},{7,15},{8,16},{9,17... | collective-permute-start | bytes 12296 | tf_op jit(solution)/shard_map/ppermute | solution.py:25
  16.8 5.4 %collective-permute-start.5 = (f32[8,128]{1,0:T(8,128)S(1)}, f32[8,128]{1,0:T(8,128)S(1)}, u32[]{:S(2)}, u32[]{:S(2)}) collective-permute-start(f32[8,128]{1,0:T(8,128)S(1)} %get-tuple-element.30), channel_id=1, source_target_pairs={{0,24},{1,25},{2,26},{3,27},{4,28},{5,29},{6,30},{7,31},{8,0},{9,1... | collective-permute-start | bytes 12296 | tf_op jit(solution)/shard_map/ppermute | solution.py:25

commit v5 on v4

--- a/solution.py
+++ b/solution.py
@@ -397,20 +397,20 @@
                 landed[row : row + 1, f * LANES : (f + 1) * LANES] = ref[3 * i + f : 3 * i + f + 1, :]
     landed[:, MASS:] = split_lanes(jnp.broadcast_to(masses, (width, LANES)))
     arrived = landed[...].astype(jnp.bfloat16)
-    chunks = sems.shape[0]
     elements = fields.shape[1]
-    per = elements // chunks
+    cuts = (0, elements // 4 * 3, elements)
     copies = []
-    for i in range(chunks):
-        rows = slice(i * per * NODES, (i + 1) * per * NODES)
-        here = slice(i * per, (i + 1) * per)
+    for i in range(len(cuts) - 1):
+        first, per = cuts[i], cuts[i + 1] - cuts[i]
+        rows = slice(first * NODES, (first + per) * NODES)
+        here = slice(first, first + per)
         total = own[rows, :] + jnp.dot(table[rows, :], arrived, preferred_element_type=jnp.float32)
         factor = 1.0 / both_halves(total[:, MASS:])
         for f in range(3):
             moved = (total[:, f * LANES : (f + 1) * LANES] * factor).reshape(per, NODES, LANES)
             held[f, here] = (fields[f, here].astype(jnp.float32) + moved).astype(jnp.bfloat16)
         copy = pltpu.make_async_copy(
-            held.at[:, pl.ds(i * per, per)], out.at[:, pl.ds(i * per, per)], sems.at[i]
+            held.at[:, pl.ds(first, per)], out.at[:, pl.ds(first, per)], sems.at[i]
         )
         copy.start()
         copies.append(copy)
@@ -496,7 +496,7 @@
         (
             vm(prognostic.shape, bf16),
             vm((plan.width, wide), f32),
-            pltpu.SemaphoreType.DMA((4,)),
+            pltpu.SemaphoreType.DMA((2,)),
         ),
     )
     return advanced

time: 23.8 us -> 23.9 us (level)
  no operation moved by 1% of the time
where the time goes in v5:
time: 23.9 us; the launch traced here: 23.7 us
  starting transfers between devices  14.4 us (60%)
  Pallas kernels  6.12 us (26%)
  waiting for transfers between devices  3.17 us (13%)
    ppermute x6, starting transfers between devices, shift(): lax.ppermute(value, AXES, [(d, (d + steps) % count) for d in range(count)])  14.4 us
    pallas_call x4, Pallas kernels, call(): pl.pallas_call(kernel, out_shape=[jax.ShapeDtypeStruct(shape, dtype) for...  6.12 us
    ppermute x6, waiting for transfers between devices, shift(): lax.ppermute(value, AXES, [(d, (d + steps) % count) for d in range(count)])  3.17 us
  transfers between devices with their start and end apart: 6, of which 2 were waited for; matrix products, arithmetic and copies ran while one was open for 0% of the time, Pallas kernels for 6%

profile of v5, /device:TPU:0, one launch (start us, length us, event | category | flops | bytes accessed | tf_op | source)
XLA Modules:
  0.0 23.7 jit_solution(14395023356476739447)
XLA Ops:
  0.0 3.2 %shard_map.64 = (bf16[3,64,16,128]{3,2,1,0:T(8,128)(2,1)S(1)}, bf16[1024,512]{1,0:T(8,128)(2,1)S(1)}, f32[8,128]{1,0:T(8,128)S(1)}, s32[16,64]{1,0:T(8,128)S(1)}...) custom-call(bf16[3,64,16,128]{3,2,1,0:T(8,128)(2,1)} %refs_0_.1, ...), custom_call_target="tpu_custom_call" | custom-call | tf_op jit(solution)/shard_map/pallas_call | solution.py:426
  3.2 3.1 %collective-permute-start.2 = (f32[296,128]{1,0:T(8,128)S(1)}, f32[296,128]{1,0:T(8,128)S(1)}, u32[]{:S(2)}, u32[]{:S(2)}) collective-permute-start(f32[296,128]{1,0:T(8,128)S(1)} %get-tuple-element.27), channel_id=1, source_target_pairs={{0,8},{1,9},{2,10},{3,11},{4,12},{5,13},{6,14},{7,15},{8,16},{9,17... | collective-permute-start | bytes 454664 | tf_op jit(solution)/shard_map/ppermute | solution.py:25
  6.3 2.1 %collective-permute-start.3 = (f32[296,128]{1,0:T(8,128)S(1)}, f32[296,128]{1,0:T(8,128)S(1)}, u32[]{:S(2)}, u32[]{:S(2)}) collective-permute-start(f32[296,128]{1,0:T(8,128)S(1)} %get-tuple-element.28), channel_id=1, source_target_pairs={{0,24},{1,25},{2,26},{3,27},{4,28},{5,29},{6,30},{7,31},{8,0},{9,1... | collective-permute-start | bytes 454664 | tf_op jit(solution)/shard_map/ppermute | solution.py:25
  8.4 1.6 %collective-permute-start = (f32[32,128]{1,0:T(8,128)S(1)}, f32[32,128]{1,0:T(8,128)S(1)}, u32[]{:S(2)}, u32[]{:S(2)}) collective-permute-start(f32[32,128]{1,0:T(8,128)S(1)} %get-tuple-element.25), channel_id=1, source_target_pairs={{0,1},{1,2},{2,3},{3,4},{4,5},{5,6},{6,7},{7,8},{8,9},{9,10},{10,1... | collective-permute-start | bytes 49160 | tf_op jit(solution)/shard_map/ppermute | solution.py:25
  10.1 3.7 %collective-permute-start.1 = (f32[32,128]{1,0:T(8,128)S(1)}, f32[32,128]{1,0:T(8,128)S(1)}, u32[]{:S(2)}, u32[]{:S(2)}) collective-permute-start(f32[32,128]{1,0:T(8,128)S(1)} %get-tuple-element.26), channel_id=1, source_target_pairs={{0,31},{1,0},{2,1},{3,2},{4,3},{5,4},{6,5},{7,6},{8,7},{9,8},{10,9... | collective-permute-start | bytes 49160 | tf_op jit(solution)/shard_map/ppermute | solution.py:25
  13.8 3.0 %collective-permute-done.refs_0_.refs_3_ = f32[32,128]{1,0:T(8,128)S(1)} collective-permute-done((f32[32,128]{1,0:T(8,128)S(1)}, f32[32,128]{1,0:T(8,128)S(1)}, u32[]{:S(2)}, u32[]{:S(2)}) %collective-permute-start) | collective-permute-done | bytes 16416 | tf_op jit(solution)/shard_map/ppermute | solution.py:25
  16.8 0.0 collective-permute-done.1.refs_1_.refs_4_
  16.8 0.1 collective-permute-start.4
  16.8 3.8 %collective-permute-start.5 = (f32[8,128]{1,0:T(8,128)S(1)}, f32[8,128]{1,0:T(8,128)S(1)}, u32[]{:S(2)}, u32[]{:S(2)}) collective-permute-start(f32[8,128]{1,0:T(8,128)S(1)} %get-tuple-element.30), channel_id=1, source_target_pairs={{0,24},{1,25},{2,26},{3,27},{4,28},{5,29},{6,30},{7,31},{8,0},{9,1... | collective-permute-start | bytes 12296 | tf_op jit(solution)/shard_map/ppermute | solution.py:25
  20.7 1.4 %shard_map.65 = (f32[1024,512]{1,0:T(8,128)S(1)}, bf16[1024,256]{1,0:T(8,128)(2,1)S(1)}) custom-call(bf16[1024,512]{1,0:T(8,128)(2,1)S(1)} %get-tuple-element.19.refs_0_, f32[8,128]{1,0:T(8,128)S(1)} %get-tuple-element.20.refs_1_, s32[16,64]{1,0:T(8,128)S(1)} %get-tuple-element.21.refs_2_, s32[1,212]{1,0:T(1,128)S(1)} %get-tuple-element.22.refs_3_), custom_call_target="tpu_custom_call" | custom-call | tf_op jit(solution)/shard_map/pallas_call | solution.py:426
  22.1 0.2 collective-permute-done.4.refs_7_
  22.2 0.0 collective-permute-done.5.refs_8_
  22.2 0.0 collective-permute-done.2.refs_5_
  22.2 0.0 collective-permute-done.3.refs_6_
  22.2 1.5 %shard_map.67 = bf16[3,64,16,128]{3,2,1,0:T(8,128)(2,1)} custom-call(bf16[3,64,16,128]{3,2,1,0:T(8,128)(2,1)S(1)} %get-tuple-element.18.refs_0_, f32[1024,512]{1,0:T(8,128)S(1)} %get-tuple-element.23.refs_1_, bf16[1024,256]{1,0:T(8,128)(2,1)S(1)} %get-tuple-element.24.refs_2_, f32[32,128]{1,0:T(8,128)S(1)} %collective-permute-done.refs_0_.refs_3_, ...), custom_call_target="tpu_custom_call" | custom-call | tf_op jit(solution)/shard_map/pallas_call | solution.py:426
  (1 shorter events, 0.0 us)
Async XLA Ops:
  3.2 19.0 %collective-permute-start.2 = (f32[296,128]{1,0:T(8,128)S(1)}, f32[296,128]{1,0:T(8,128)S(1)}, u32[]{:S(2)}, u32[]{:S(2)}) collective-permute-start(f32[296,128]{1,0:T(8,128)S(1)} %get-tuple-element.27), channel_id=1, source_target_pairs={{0,8},{1,9},{2,10},{3,11},{4,12},{5,13},{6,14},{7,15},{8,16},{9,17... | collective-permute-start | bytes 454664 | tf_op jit(solution)/shard_map/ppermute | solution.py:25
  6.3 15.9 %collective-permute-start.3 = (f32[296,128]{1,0:T(8,128)S(1)}, f32[296,128]{1,0:T(8,128)S(1)}, u32[]{:S(2)}, u32[]{:S(2)}) collective-permute-start(f32[296,128]{1,0:T(8,128)S(1)} %get-tuple-element.28), channel_id=1, source_target_pairs={{0,24},{1,25},{2,26},{3,27},{4,28},{5,29},{6,30},{7,31},{8,0},{9,1... | collective-permute-start | bytes 454664 | tf_op jit(solution)/shard_map/ppermute | solution.py:25
  8.4 8.3 %collective-permute-start = (f32[32,128]{1,0:T(8,128)S(1)}, f32[32,128]{1,0:T(8,128)S(1)}, u32[]{:S(2)}, u32[]{:S(2)}) collective-permute-start(f32[32,128]{1,0:T(8,128)S(1)} %get-tuple-element.25), channel_id=1, source_target_pairs={{0,1},{1,2},{2,3},{3,4},{4,5},{5,6},{6,7},{7,8},{8,9},{9,10},{10,1... | collective-permute-start | bytes 49160 | tf_op jit(solution)/shard_map/ppermute | solution.py:25
  10.1 6.7 %collective-permute-start.1 = (f32[32,128]{1,0:T(8,128)S(1)}, f32[32,128]{1,0:T(8,128)S(1)}, u32[]{:S(2)}, u32[]{:S(2)}) collective-permute-start(f32[32,128]{1,0:T(8,128)S(1)} %get-tuple-element.26), channel_id=1, source_target_pairs={{0,31},{1,0},{2,1},{3,2},{4,3},{5,4},{6,5},{7,6},{8,7},{9,8},{10,9... | collective-permute-start | bytes 49160 | tf_op jit(solution)/shard_map/ppermute | solution.py:25
  16.8 5.5 %collective-permute-start.4 = (f32[8,128]{1,0:T(8,128)S(1)}, f32[8,128]{1,0:T(8,128)S(1)}, u32[]{:S(2)}, u32[]{:S(2)}) collective-permute-start(f32[8,128]{1,0:T(8,128)S(1)} %get-tuple-element.29), channel_id=1, source_target_pairs={{0,8},{1,9},{2,10},{3,11},{4,12},{5,13},{6,14},{7,15},{8,16},{9,17... | collective-permute-start | bytes 12296 | tf_op jit(solution)/shard_map/ppermute | solution.py:25
  16.8 5.4 %collective-permute-start.5 = (f32[8,128]{1,0:T(8,128)S(1)}, f32[8,128]{1,0:T(8,128)S(1)}, u32[]{:S(2)}, u32[]{:S(2)}) collective-permute-start(f32[8,128]{1,0:T(8,128)S(1)} %get-tuple-element.30), channel_id=1, source_target_pairs={{0,24},{1,25},{2,26},{3,27},{4,28},{5,29},{6,30},{7,31},{8,0},{9,1... | collective-permute-start | bytes 12296 | tf_op jit(solution)/shard_map/ppermute | solution.py:25
